TPU v7x, 128 devices: a whole 4x4x4 slice. The times are simulated.
128 devices in a mesh: band: 8 (over y, x_lo), chan: 16 (over x_hi, z, core).
Axes of the slice: x: 4 (x_hi: 2, x_lo: 2; x = x_hi * 2 + x_lo), y: 4, z: 4, core: 2. Of those that a mesh axis runs over, the one named last changes fastest.
Arguments:
- coeffs: bfloat16 [2, 8, 1024, 8192], P(None, None, 'chan', 'band'), may hold values from -1100 to 1100, as said below
Outputs:
- coherence: float32 [1024, 1024], P('chan', 'band')
Inputs may be any that keep to these rules, and one draw needn't show every extreme that they name: `coeffs`: finite real and imaginary parts.
All inputs are finite; a program needn't handle non-finite values.
Results may differ from a plain program's by a relative error of at most 0.0003.
Values may be sent and summed in bfloat16 or wider, within the bound.
No kernel may reach another device: no remote copies, remote signals or barrier semaphores. Data moves between devices by JAX's collectives and lax.ppermute only.
A program may use at most 192 MiB of HBM per device.

v0:
```python
import jax
import jax.numpy as jnp
from jax import lax
from jax.sharding import PartitionSpec as P

K = 8
W = 16


epsilon = 1e-06


def in_blocks(shard, dim, length):
    dims = shard.shape
    tiles = shard.reshape(*dims[:dim], length, dims[dim] // length, *dims[dim + 1 :])
    return jnp.moveaxis(tiles, dim, 0)


def sent_and_summed(shard, axis, dim):
    length = lax.axis_size(axis)
    tiles = lax.all_to_all(in_blocks(shard, dim, length), axis, 0, 0, tiled=True)
    return jnp.sum(tiles, axis=0)


def body(coeffs):
    num_bands = coeffs.shape[3] // W
    own_width = coeffs.shape[2]
    cycle_size = lax.axis_size("chan")
    own_index = lax.axis_index("chan")
    full_width = own_width * cycle_size
    group_count = lax.axis_size("band")
    scale = jnp.float32(W * K / (num_bands * group_count))
    local_rows = coeffs.reshape(2, K, own_width, num_bands, W)
    paired = jnp.stack((local_rows[1], -local_rows[0]), axis=0)
    left_side = jnp.concatenate((local_rows, paired), axis=2)
    wide_rows = local_rows.astype(jnp.float32)
    own_power = jnp.sum(wide_rows * wide_rows, axis=(0, 1, 4)).T + epsilon
    piece = lax.all_gather(coeffs, "chan", axis=2, tiled=True)
    count = piece.shape[2]
    right_side = piece.reshape(2, K, count, num_bands, W)
    product = jnp.einsum(
        "pkinw,pkjnw->nij", left_side, right_side, preferred_element_type=jnp.float32
    )
    real_part = product[:, :own_width, :]
    imag_part = product[:, own_width:, :]
    wide_piece = right_side.astype(jnp.float32)
    piece_power = jnp.sum(wide_piece * wide_piece, axis=(0, 1, 4)).T + epsilon
    coh_band = (real_part * real_part + imag_part * imag_part) / (
        own_power[:, :, None] * piece_power[:, None, :]
    )
    partial_value = jnp.sum(coh_band, axis=0)
    row_global = lax.broadcasted_iota(jnp.int32, (own_width, full_width), 0) + own_index * own_width
    col_global = lax.broadcasted_iota(jnp.int32, (own_width, full_width), 1)
    partial_value = jnp.where(row_global == col_global, jnp.float32(0.0), partial_value)
    result = sent_and_summed(partial_value, "band", 1)
    return result * scale


def solution(mesh):
    return jax.shard_map(
        body,
        mesh=mesh,
        in_specs=(P(None, None, "chan", "band"),),
        out_specs=P("chan", "band"),
        check_vma=False,
    )
```

profile of v0, /device:TPU:0, one launch (start us, length us, event | category | flops | bytes accessed | tf_op | source)
XLA Modules:
  0.0 327.6 jit_solution(6133088543758207707)
XLA Ops:
  6.5 0.0 copy-start
  6.5 0.0 all-gather.2.cloned.1.call-start
  6.5 4.2 %copy.37 = bf16[2,8,64,1024]{3,1,0,2:T(8,128)(2,1)} copy(bf16[2,8,64,1024]{3,2,1,0:T(8,128)(2,1)} %param.1) | data formatting | bytes 4194304 | tf_op args[0]
  10.7 0.0 all-gather.2.cloned.1.call-update
  10.8 0.0 copy-done
  10.8 3.2 copy.31
  14.0 0.4 multiply_reduce_fusion.1
  14.4 0.2 copy.40
  14.6 0.1 bitcast_reduce_fusion.1
  14.7 4.0 %fusion.14 = (bf16[1,8,64,1024]{2,3,1,0:T(8,128)(2,1)S(1)}, bf16[1,8,64,1024]{2,3,1,0:T(8,128)(2,1)}) fusion(bf16[2,8,64,1024]{2,3,1,0:T(8,128)(2,1)} %copy.31), kind=kLoop, calls=%fused_computation.25 | loop fusion | flops 524288 | bytes 4194304 | tf_op jit(solution)/shard_map/slice | solution.py:34
  18.7 180.3 %all-gather.2.cloned.1.call-done = bf16[2,8,1024,1024]{3,1,0,2:T(8,128)(2,1)} async-done(((bf16[2,8,64,1024]{3,1,0,2:T(8,128)(2,1)}), bf16[2,8,1024,1024]{3,1,0,2:T(8,128)(2,1)}) %all-gather.2.cloned.1.call-update) | async-done | bytes 33554448 | tf_op jit(solution)/shard_map/all_gather | solution.py:38
  199.1 18.3 %multiply_reduce_fusion = f32[1024,1024]{1,0:T(8,128)} fusion(bf16[2,8,1024,1024]{3,1,0,2:T(8,128)(2,1)} %all-gather.2.cloned.1.call-done), kind=kLoop, calls=%fused_computation | loop fusion | flops 49283072 | bytes 37748736 | tf_op jit(solution)/shard_map/reduce_sum | solution.py:47
  217.3 5.3 %copy.41 = f32[1024,1024]{0,1:T(8,128)} copy(f32[1024,1024]{1,0:T(8,128)} %multiply_reduce_fusion) | data formatting | bytes 8388608 | tf_op jit(solution)/shard_map/reduce_sum | solution.py:47
  222.7 3.1 bitcast_reduce_fusion
  225.8 45.1 %copy.38 = bf16[2,8,1024,1024]{2,3,1,0:T(8,128)(2,1)} copy(bf16[2,8,1024,1024]{3,1,0,2:T(8,128)(2,1)} %all-gather.2.cloned.1.call-done) | data formatting | bytes 67108864 | tf_op jit(solution)/shard_map/all_gather | solution.py:38
  271.0 25.2 %fusion.5 = f32[64,128,1024]{2,1,0:T(8,128)} fusion(bf16[2,8,1024,64,16]{2,4,3,1,0:T(8,128)(2,1)} %bitcast.24, bf16[1,8,64,64,16]{2,4,0,3,1:T(8,128)(2,1)} %bitcast.27, bf16[1,8,64,64,16]{2,4,0,3,1:T(8,128)(2,1)S(1)} %bitcast.26, bf16[2,8,64,64,16]{2,4,3,1,0:T(8,128)(2,1)} %bitcast.25), kind=kOutput, calls=%fused_computation.8 | convolution fusion | flops 4307550208 | bytes 71303168 | tf_op jit(solution)/shard_map/pkinw,pkjnw->nij/dot_general | solution.py:41
  296.2 11.9 %fusion.4 = f32[64,1024]{1,0:T(8,128)S(1)} fusion(f32[64,128,1024]{2,1,0:T(8,128)} %fusion.5, f32[64,1024]{1,0:T(8,128)S(1)} %add_bitcast_fusion, f32[64,64]{1,0:T(8,128)S(1)} %add_bitcast_fusion.1), kind=kLoop, calls=%fused_computation.7 | loop fusion | flops 25100288 | bytes 34095104 | tf_op jit(solution)/shard_map/reduce_sum | solution.py:51
  308.1 0.1 bitcast_select_fusion
  308.3 0.1 copy.42
  308.3 11.8 %all_to_all.5 = f32[8,64,128]{2,1,0:T(8,128)S(1)} all-to-all(f32[8,64,128]{2,1,0:T(8,128)S(1)} %copy.42), channel_id=1, replica_groups=mesh['band'=8,'chan'=16] {'band'}, dimensions={0} | all-to-all | bytes 524288 | tf_op jit(solution)/shard_map/all_to_all | solution.py:21
  320.1 0.6 broadcast_multiply_fusion
  (6 shorter events, 0.1 us)
Async XLA Ops:
  6.5 4.2 %copy-start = (bf16[2,8,64,1024]{3,2,1,0:T(8,128)(2,1)S(1)}, bf16[2,8,64,1024]{3,2,1,0:T(8,128)(2,1)}, u32[]{:S(2)}) copy-start(bf16[2,8,64,1024]{3,2,1,0:T(8,128)(2,1)} %param.1) | copy-start | bytes 6291460
  6.5 192.5 %all-gather.2.cloned.1.call-start = ((), (), s32[]{:S(2)}) async-start(), calls=%async_computation.1 | async-start | bytes 35651584 | tf_op jit(solution)/shard_map/all_gather | solution.py:38
Sparse Core Ops, SparseCore 0:
  10.9 188.1 all-gather.1
where the time goes:
time: 329 us; the launch traced here: 328 us
  waiting for transfers between devices  180 us (55%)
  local copies, waits for them, and re-layouts  58.2 us (18%)
  other arithmetic  38.6 us (12%)
  matrix products  25.2 us (8%)
  between operations  13.5 us (4%)
  blocking collectives  11.8 us (4%)
    all_gather x1, waiting for transfers between devices, body(): piece = lax.all_gather(coeffs, 'chan', axis=2, tiled=True)  180 us
    all_gather x1, local copies, waits for them, and re-layouts, body(): piece = lax.all_gather(coeffs, 'chan', axis=2, tiled=True)  45.1 us
    dot_general x1, matrix products, body(): jnp.einsum('pkinw,pkjnw->nij', left_side, right_side, preferred_element_t...  25.2 us
    reduce_sum x2, other arithmetic, body(): piece_power = jnp.sum(wide_piece * wide_piece, axis=(0, 1, 4)).T + epsilon  21.4 us
    reduce_sum x1, other arithmetic, body(): partial_value = jnp.sum(coh_band, axis=0)  11.9 us
    all_to_all x1, blocking collectives, sent_and_summed(): lax.all_to_all(in_blocks(shard, dim, length), axis, 0, 0, tiled=True)  11.8 us
    unnamed x5, local copies, waits for them, and re-layouts  7.43 us
  transfers between devices with their start and end apart: 1, of which 1 were waited for; matrix products, arithmetic and copies ran while one was open for 2% of the time, Pallas kernels for 0%

commit v1 on v0

v1 whole, which is shorter than its diff:
```python
import jax
import jax.numpy as jnp
from jax import lax
from jax.experimental import pallas as pl
from jax.experimental.pallas import tpu as pltpu
from jax.sharding import Mesh, PartitionSpec as P

K = 8
W = 16
EPS = 1e-06


def turn_kernel(x_ref, o_ref):
    tiles = x_ref.shape[3] // 128
    for t in range(tiles):
        re = x_ref[0, 0, :, t * 128 : (t + 1) * 128]
        im = x_ref[1, 0, :, t * 128 : (t + 1) * 128]
        both = jnp.concatenate((re, im), axis=0).T
        o_ref[2 * t, 0] = both[:64]
        o_ref[2 * t + 1, 0] = both[64:]


def turned(coeffs):
    width, bins = coeffs.shape[2:]
    return pl.pallas_call(
        turn_kernel,
        grid=(K,),
        in_specs=[pl.BlockSpec((2, 1, width, bins), lambda k: (0, k, 0, 0))],
        out_specs=pl.BlockSpec((bins // 64, 1, 64, 128), lambda k: (0, k, 0, 0)),
        out_shape=jax.ShapeDtypeStruct((bins // 64, K, 64, 128), jnp.bfloat16),
    )(coeffs)


BANDS = 4


def pair_kernel(core_ref, x_ref, own_ref, other_ref, right, left, row_inv, col_inv):
    core = core_ref[0]
    low = lax.broadcasted_iota(jnp.int32, (BANDS * W, 128), 1) < 64
    for s in range(8):
        lanes = slice(s * 128, (s + 1) * 128)
        for k in range(K):
            a = x_ref[2 * s, k]
            b = x_ref[2 * s + 1, k]
            a_turned = jnp.concatenate((a[:, 64:], a[:, :64]), axis=1)
            b_turned = jnp.concatenate((b[:, 64:], b[:, :64]), axis=1)
            re = jnp.where(low, a, b_turned)
            im = jnp.where(low, a_turned, b)
            for n in range(BANDS):
                right[n, k * W : (k + 1) * W, lanes] = re[n * W : (n + 1) * W]
                right[n, 128 + k * W : 128 + (k + 1) * W, lanes] = im[n * W : (n + 1) * W]

    def prepare(i, carry):
        n = i // 8
        s = i % 8
        block = right[n, :, pl.ds(pl.multiple_of(s * 128, 128), 128)]
        wide = block.astype(jnp.float32)
        power = jnp.sum(wide * wide, axis=0, keepdims=True) + EPS
        inv = 1.0 / power
        row_inv[n, :, pl.ds(pl.multiple_of(s * 128, 128), 128)] = jnp.broadcast_to(inv, (8, 128))
        rows = pl.ds(pl.multiple_of(s * 128, 128), 128)
        turned = block.T
        left[0, n, rows, :] = turned
        left[1, n, rows, 0:128] = turned[:, 128:]
        left[1, n, rows, 128:256] = -turned[:, :128]
        col_inv[n, rows, :] = jnp.broadcast_to(inv, (128, 128)).T
        return carry

    lax.fori_loop(0, BANDS * 8, prepare, 0)

    def tile(s, carry):
        for half in range(2):
            out_ref = (own_ref, other_ref)[half]
            c = core if half == 0 else 1 - core
            rows = pl.ds(pl.multiple_of(s * 128 + c * 64, 64), 64)
            for j in range(4):
                cols = slice(j * 256, (j + 1) * 256)
                total = jnp.zeros((64, 256), jnp.float32)
                for n in range(BANDS):
                    lhs = jnp.concatenate((left[0, n, rows, :], left[1, n, rows, :]), axis=0)
                    both = jnp.dot(lhs, right[n, :, cols], preferred_element_type=jnp.float32)
                    re = both[:64]
                    im = both[64:]
                    ci = col_inv[n, rows, :]
                    ci = jnp.concatenate((ci, ci), axis=1)
                    total += (re * re + im * im) * row_inv[n, 0:1, cols] * ci
                out_ref[s, :, cols] = total
        return carry

    lax.fori_loop(0, 8, tile, 0)


def pairs(core, x):
    shape = jax.ShapeDtypeStruct((8, 64, 1024), jnp.float32)
    return pl.pallas_call(
        pair_kernel,
        in_specs=[
            pl.BlockSpec(memory_space=pltpu.SMEM),
            pl.BlockSpec(memory_space=pltpu.VMEM),
        ],
        out_specs=[pl.BlockSpec(memory_space=pltpu.VMEM)] * 2,
        out_shape=[shape, shape],
        scratch_shapes=[
            pltpu.VMEM((BANDS, 256, 1024), jnp.bfloat16),
            pltpu.VMEM((2, BANDS, 1024, 256), jnp.bfloat16),
            pltpu.VMEM((BANDS, 8, 1024), jnp.float32),
            pltpu.VMEM((BANDS, 1024, 128), jnp.float32),
        ],
        compiler_params=pltpu.CompilerParams(vmem_limit_bytes=40 * 2**20),
    )(core, x)


def add_kernel(a_ref, b_ref, o_ref):
    for g in range(8):
        cols = slice(g * 128, (g + 1) * 128)
        o_ref[g] = a_ref[:, :, cols] + b_ref[:, :, cols]


def added(a, b):
    return pl.pallas_call(
        add_kernel,
        in_specs=[pl.BlockSpec(memory_space=pltpu.VMEM)] * 2,
        out_specs=pl.BlockSpec(memory_space=pltpu.VMEM),
        out_shape=jax.ShapeDtypeStruct((8, 8, 64, 128), jnp.float32),
    )(a, b)


def body(scale, coeffs):
    core = lax.axis_index("core")
    chan = lax.axis_index("chip") * 2 + core
    band = lax.axis_index("band")
    sent = turned(coeffs)
    mine = lax.all_to_all(sent, ("chip", "core"), 0, 0, tiled=True)
    own, other = pairs(core.astype(jnp.int32).reshape(1), mine)
    other = lax.ppermute(other, "core", [(0, 1), (1, 0)])
    blocks = added(own, other).reshape(64, 64, 128)
    blocks = lax.all_to_all(blocks, ("band", "chip"), 0, 0, tiled=True)
    total = jnp.sum(blocks, axis=0) * scale
    row = lax.broadcasted_iota(jnp.int32, (64, 128), 0) + chan * 64
    col = lax.broadcasted_iota(jnp.int32, (64, 128), 1) + band * 128
    return jnp.where(row == col, jnp.float32(0.0), total)


def solution(mesh):
    fine = Mesh(mesh.devices.reshape(8, 8, 2), ("band", "chip", "core"))
    scale = W * K / 512

    def whole(coeffs):
        return jax.shard_map(
            lambda x: body(scale, x),
            mesh=fine,
            in_specs=(P(None, None, ("chip", "core"), "band"),),
            out_specs=P(("chip", "core"), "band"),
            check_vma=False,
        )(coeffs)

    return whole
```

time: 329 us -> 108 us (0.33)
  waiting for transfers between devices: 180 us -> 63.4 us
  local copies, waits for them, and re-layouts: 58.2 us -> 2.63 us
  other arithmetic: 38.6 us -> 0.84 us
  matrix products: 25.2 us -> 0 us
  Pallas kernels: 0 us -> 23.3 us
  starting transfers between devices: 0.01 us -> 17.6 us
  between operations: 13.5 us -> 0.06 us
  blocking collectives: 11.8 us -> 0 us
    all_gather x1 -> x0, waiting for transfers between devices: 180 us -> none  [body(): piece = lax.all_gather(coeffs, 'chan', axis=2, tiled=True)]
    all_to_all x0 -> x2, waiting for transfers between devices: none -> 59.3 us  [the longest x1 30 us: body(): blocks = lax.all_to_all(blocks, ('band', 'chip'), 0, 0, tiled=True)]
    all_gather x1 -> x0, local copies, waits for them, and re-layouts: 45.1 us -> none  [body(): piece = lax.all_gather(coeffs, 'chan', axis=2, tiled=True)]
    reduce_sum x6 -> x1, other arithmetic: 33.8 us -> 0.14 us  [body(): total = jnp.sum(blocks, axis=0) * scale]
    dot_general x1 -> x0, matrix products: 25.2 us -> none  [body(): jnp.einsum('pkinw,pkjnw->nij', left_side, right_side, preferred_element_t...]
    pallas_call x0 -> x3, Pallas kernels: none -> 23.3 us  [the longest x1 13.2 us: pairs(): pl.pallas_call(pair_kernel, in_specs=[pl.BlockSpec(memory_space=pltpu.SME...]
    all_to_all x0 -> x2, starting transfers between devices: none -> 17.5 us  [the longest x1 9.56 us: body(): blocks = lax.all_to_all(blocks, ('band', 'chip'), 0, 0, tiled=True)]
    all_to_all x1 -> x0, blocking collectives: 11.8 us -> none  [sent_and_summed(): lax.all_to_all(in_blocks(shard, dim, length), axis, 0, 0, tiled=True)]
  transfers between devices with their start and end apart: 1 -> 3, of which waited for: 1 -> 3; matrix products, arithmetic and copies ran while one was open for 2% -> 0% of each run, Pallas kernels for 0% -> 0%
where the time goes in v1:
time: 108 us
  waiting for transfers between devices  63.4 us (59%)
  Pallas kernels  23.3 us (22%)
  starting transfers between devices  17.6 us (16%)
  local copies, waits for them, and re-layouts  2.63 us (2%)
    all_to_all x1, waiting for transfers between devices, body(): blocks = lax.all_to_all(blocks, ('band', 'chip'), 0, 0, tiled=True)  30 us
    all_to_all x1, waiting for transfers between devices, body(): mine = lax.all_to_all(sent, ('chip', 'core'), 0, 0, tiled=True)  29.3 us
    pallas_call x1, Pallas kernels, pairs(): pl.pallas_call(pair_kernel, in_specs=[pl.BlockSpec(memory_space=pltpu.SME...  13.2 us
    all_to_all x1, starting transfers between devices, body(): blocks = lax.all_to_all(blocks, ('band', 'chip'), 0, 0, tiled=True)  9.56 us
    all_to_all x1, starting transfers between devices, body(): mine = lax.all_to_all(sent, ('chip', 'core'), 0, 0, tiled=True)  7.99 us
    pallas_call x1, Pallas kernels, turned(): pl.pallas_call(turn_kernel, grid=(K,), in_specs=[pl.BlockSpec((2, 1, widt...  6.09 us
    ppermute x1, waiting for transfers between devices, body(): other = lax.ppermute(other, 'core', [(0, 1), (1, 0)])  4.16 us
    pallas_call x1, Pallas kernels, added(): pl.pallas_call(add_kernel, in_specs=[pl.BlockSpec(memory_space=pltpu.VMEM...  3.95 us
  transfers between devices with their start and end apart: 3, of which 3 were waited for; matrix products, arithmetic and copies ran while one was open for 0% of the time, Pallas kernels for 0%

profile of v1, /device:TPU:0, one launch (start us, length us, event | category | flops | bytes accessed | tf_op | source)
XLA Modules:
  0.0 107.8 jit_solution(11675316213971958243)
XLA Ops:
  0.0 6.1 %shard_map.17 = bf16[16,8,64,128]{3,2,1,0:T(8,128)(2,1)} custom-call(bf16[2,8,64,1024]{3,2,1,0:T(8,128)(2,1)} %x_ref.1), custom_call_target="tpu_custom_call" | custom-call | tf_op jit(solution)/shard_map/pallas_call | solution.py:25
  6.1 8.0 %all-to-all-start = ((bf16[16,8,64,128]{3,2,1,0:T(8,128)(2,1)}), bf16[16,8,64,128]{3,2,1,0:T(8,128)(2,1)S(1)}, u32[]{:S(2)}, u32[]{:S(2)}) async-start(bf16[16,8,64,128]{3,2,1,0:T(8,128)(2,1)} %shard_map.17), calls=%async_computation | async-start | bytes 4194304 | tf_op jit(solution)/shard_map/all_to_all | solution.py:133
  14.1 29.3 %all-to-all-done.x_ref = bf16[16,8,64,128]{3,2,1,0:T(8,128)(2,1)S(1)} async-done(((bf16[16,8,64,128]{3,2,1,0:T(8,128)(2,1)}), bf16[16,8,64,128]{3,2,1,0:T(8,128)(2,1)S(1)}, u32[]{:S(2)}, u32[]{:S(2)}) %all-to-all-start) | async-done | bytes 2097184 | tf_op jit(solution)/shard_map/all_to_all | solution.py:133
  43.4 13.2 %shard_map.18 = (f32[8,64,1024]{2,1,0:T(8,128)S(1)}, f32[8,64,1024]{2,1,0:T(8,128)S(1)}) custom-call(s32[1]{0:T(128)} %bitcast.core_ref, bf16[16,8,64,128]{3,2,1,0:T(8,128)(2,1)S(1)} %all-to-all-done.x_ref), custom_call_target="tpu_custom_call" | custom-call | tf_op jit(solution)/shard_map/pallas_call | solution.py:95
  56.6 0.0 copy-start
  56.6 1.3 %copy-done = f32[8,64,1024]{2,1,0:T(8,128)} copy-done((f32[8,64,1024]{2,1,0:T(8,128)}, f32[8,64,1024]{2,1,0:T(8,128)S(1)}, u32[]{:S(2)}) %copy-start) | copy-done | bytes 2097176
  57.9 0.0 collective-permute-start
  57.9 4.2 %collective-permute-done.b_ref = f32[8,64,1024]{2,1,0:T(8,128)S(1)} collective-permute-done((f32[8,64,1024]{2,1,0:T(8,128)S(1)}, f32[8,64,1024]{2,1,0:T(8,128)S(1)}, u32[]{:S(2)}, u32[]{:S(2)}) %collective-permute-start) | collective-permute-done | bytes 2097184 | tf_op jit(solution)/shard_map/ppermute | solution.py:135
  62.1 0.0 copy-start.1
  62.1 1.3 %copy-done.1 = f32[8,64,1024]{2,1,0:T(8,128)} copy-done((f32[8,64,1024]{2,1,0:T(8,128)}, f32[8,64,1024]{2,1,0:T(8,128)S(1)}, u32[]{:S(2)}) %copy-start.1) | copy-done | bytes 2097176
  63.4 4.0 %shard_map.19 = f32[8,8,64,128]{3,2,1,0:T(8,128)} custom-call(f32[8,64,1024]{2,1,0:T(8,128)} %copy-done, f32[8,64,1024]{2,1,0:T(8,128)} %copy-done.1), custom_call_target="tpu_custom_call" | custom-call | tf_op jit(solution)/shard_map/pallas_call | solution.py:120
  67.3 9.6 %all-to-all-start.1 = ((f32[64,64,128]{2,1,0:T(8,128)}), f32[64,64,128]{2,1,0:T(8,128)S(1)}, u32[]{:S(2)}, u32[]{:S(2)}) async-start(f32[64,64,128]{2,1,0:T(8,128)} %bitcast.2), calls=%async_computation.1 | async-start | bytes 4194304 | tf_op jit(solution)/shard_map/all_to_all | solution.py:137
  76.9 30.0 %all-to-all-done.1 = f32[64,64,128]{2,1,0:T(8,128)S(1)} async-done(((f32[64,64,128]{2,1,0:T(8,128)}), f32[64,64,128]{2,1,0:T(8,128)S(1)}, u32[]{:S(2)}, u32[]{:S(2)}) %all-to-all-start.1) | async-done | bytes 2097184 | tf_op jit(solution)/shard_map/all_to_all | solution.py:137
  107.0 0.1 reduce_sum.9
  107.1 0.7 multiply_select_fusion
  (2 shorter events, 0.0 us)
Async XLA Ops:
  6.1 37.3 %all-to-all-start = ((bf16[16,8,64,128]{3,2,1,0:T(8,128)(2,1)}), bf16[16,8,64,128]{3,2,1,0:T(8,128)(2,1)S(1)}, u32[]{:S(2)}, u32[]{:S(2)}) async-start(bf16[16,8,64,128]{3,2,1,0:T(8,128)(2,1)} %shard_map.17), calls=%async_computation | async-start | bytes 4194304 | tf_op jit(solution)/shard_map/all_to_all | solution.py:133
  56.6 1.3 %copy-start = (f32[8,64,1024]{2,1,0:T(8,128)}, f32[8,64,1024]{2,1,0:T(8,128)S(1)}, u32[]{:S(2)}) copy-start(f32[8,64,1024]{2,1,0:T(8,128)S(1)} %get-tuple-element.7.a_ref) | copy-start | bytes 6291460
  57.9 4.2 %collective-permute-start = (f32[8,64,1024]{2,1,0:T(8,128)S(1)}, f32[8,64,1024]{2,1,0:T(8,128)S(1)}, u32[]{:S(2)}, u32[]{:S(2)}) collective-permute-start(f32[8,64,1024]{2,1,0:T(8,128)S(1)} %get-tuple-element.8), channel_id=1, source_target_pairs={{0,1},{1,0},{2,3},{3,2},{4,5},{5,4},{6,7},{7,6},{8,9},{9,8},{10,11... | collective-permute-start | bytes 6291464 | tf_op jit(solution)/shard_map/ppermute | solution.py:135
  62.1 1.3 %copy-start.1 = (f32[8,64,1024]{2,1,0:T(8,128)}, f32[8,64,1024]{2,1,0:T(8,128)S(1)}, u32[]{:S(2)}) copy-start(f32[8,64,1024]{2,1,0:T(8,128)S(1)} %collective-permute-done.b_ref) | copy-start | bytes 6291460
  67.3 39.6 %all-to-all-start.1 = ((f32[64,64,128]{2,1,0:T(8,128)}), f32[64,64,128]{2,1,0:T(8,128)S(1)}, u32[]{:S(2)}, u32[]{:S(2)}) async-start(f32[64,64,128]{2,1,0:T(8,128)} %bitcast.2), calls=%async_computation.1 | async-start | bytes 4194304 | tf_op jit(solution)/shard_map/all_to_all | solution.py:137

commit v2 on v0

v2 whole, which is shorter than its diff:
```python
import jax
import jax.numpy as jnp
from jax import lax
from jax.experimental import pallas as pl
from jax.experimental.pallas import tpu as pltpu
from jax.sharding import Mesh, PartitionSpec as P

K = 8
W = 16
EPS = 1e-06
CHUNKS = (8,)

LIMIT = 2.0**-11
SQUARE = 2.0**8
LINEAR = 2.0**26

WHOLE = pl.BlockSpec(memory_space=pltpu.VMEM)
SCALAR = pl.BlockSpec(memory_space=pltpu.SMEM)


def turn_kernel(core_ref, x_ref, *refs):
    outs = refs[: len(CHUNKS)]
    buffer, sems = refs[len(CHUNKS) :]
    core = core_ref[0]

    def fetch(k):
        return pltpu.make_async_copy(x_ref.at[:, k], buffer.at[k], sems.at[k])

    for k in range(K):
        fetch(k).start()

    def step(k, carry):
        fetch(k).wait()
        for t in range(8):
            lanes = slice(t * 128, (t + 1) * 128)
            first = buffer[k, core, :, lanes]
            second = buffer[k, 1 - core, :, lanes]
            both = jnp.concatenate((first, second), axis=0).T
            start = 0
            for o_ref, bands in zip(outs, CHUNKS):
                o_ref[t, k] = both[start : start + bands * W]
                start += bands * W
        return carry

    lax.fori_loop(0, K, step, 0)


def turned(core, coeffs):
    width, bins = coeffs.shape[2:]
    return pl.pallas_call(
        turn_kernel,
        in_specs=[SCALAR, pl.BlockSpec(memory_space=pltpu.HBM)],
        out_specs=[WHOLE] * len(CHUNKS),
        out_shape=[
            jax.ShapeDtypeStruct((8, K, bands * W, 128), jnp.bfloat16) for bands in CHUNKS
        ],
        scratch_shapes=[
            pltpu.VMEM((K, 2, width, bins), jnp.bfloat16),
            pltpu.SemaphoreType.DMA((K,)),
        ],
        compiler_params=pltpu.CompilerParams(vmem_limit_bytes=10 * 2**20),
    )(core, coeffs)


def left_kernel(core_ref, x_ref, left, col_inv):
    core = core_ref[0]
    bands = x_ref.shape[2] // W
    for n in range(bands):
        for s in range(8):
            block = jnp.concatenate(
                [x_ref[s, k, n * W : (n + 1) * W, :] for k in range(K)], axis=0
            )
            turned = block.T
            first = turned[:64]
            second = turned[64:]
            re = jnp.where(core == 0, first, second)
            im = jnp.where(core == 0, second, first)
            rows = slice(s * 64, (s + 1) * 64)
            left[0, n, rows, 0:128] = re
            left[0, n, rows, 128:256] = im
            left[1, n, rows, 0:128] = im
            left[1, n, rows, 128:256] = -re
            wide = block.astype(jnp.float32)
            halves = jnp.sum(wide * wide, axis=0, keepdims=True)
            power = halves + jnp.concatenate((halves[:, 64:], halves[:, :64]), axis=1)
            inv = 1.0 / (power + EPS)
            col_inv[n, rows, :] = jnp.broadcast_to(inv, (128, 128)).T[:64]


def lefts(core, x):
    bands = x.shape[2] // W
    return pl.pallas_call(
        left_kernel,
        in_specs=[SCALAR, WHOLE],
        out_specs=[WHOLE] * 2,
        out_shape=[
            jax.ShapeDtypeStruct((2, bands, 512, 256), jnp.bfloat16),
            jax.ShapeDtypeStruct((bands, 512, 128), jnp.float32),
        ],
        compiler_params=pltpu.CompilerParams(vmem_limit_bytes=16 * 2**20),
    )(core, x)


def pair_kernel(bands, first, last, core_ref, own_ref, other_ref, left, col_inv, *refs):
    refs = list(refs)
    before = None if first else refs.pop(0)
    o_ref, right, row_inv = refs
    core = core_ref[0]
    lane = lax.broadcasted_iota(jnp.int32, (bands * W, 128), 1)
    mine = (lane < 64) == (core == 0)
    for s in range(8):
        lanes = slice(s * 128, (s + 1) * 128)
        for k in range(K):
            own = own_ref[s, k]
            other = other_ref[s, k]
            re = jnp.where(mine, own, other)
            im = jnp.where(mine, other, own)
            im = jnp.concatenate((im[:, 64:], im[:, :64]), axis=1)
            for n in range(bands):
                right[n, k * W : (k + 1) * W, lanes] = re[n * W : (n + 1) * W]
                right[n, 128 + k * W : 128 + (k + 1) * W, lanes] = im[n * W : (n + 1) * W]

    for n in range(bands):
        for s in range(8):
            lanes = slice(s * 128, (s + 1) * 128)
            wide = right[n, :, lanes].astype(jnp.float32)
            power = jnp.sum(wide * wide, axis=0, keepdims=True) + EPS
            row_inv[n, :, lanes] = jnp.broadcast_to(1.0 / power, (8, 128))

    def tile(i, carry):
        rows = pl.ds(pl.multiple_of(i * 128, 128), 128)
        for j in range(4):
            cols = slice(j * 256, (j + 1) * 256)
            total = jnp.zeros((128, 256), jnp.float32)
            for n in range(bands):
                lhs = jnp.concatenate((left[0, n, rows, :], left[1, n, rows, :]), axis=0)
                both = jnp.dot(lhs, right[n, :, cols], preferred_element_type=jnp.float32)
                re = both[:128]
                im = both[128:]
                ci = col_inv[n, rows, :]
                ci = jnp.concatenate((ci, ci), axis=1)
                total += (re * re + im * im) * row_inv[n, 0:1, cols] * ci
            if before is not None:
                total += before[rows, cols]
            if last:
                coded = jnp.where(total >= LIMIT, total * total * SQUARE, total * -LINEAR)
                for h in range(2):
                    for g in range(2):
                        o_ref[2 * j + g, 2 * i + h] = coded[
                            h * 64 : (h + 1) * 64, g * 128 : (g + 1) * 128
                        ]
            else:
                o_ref[rows, cols] = total
        return carry

    lax.fori_loop(0, 4, tile, 0)


def pairs(core, own, other, left, col_inv, before, last):
    bands = own.shape[2] // W
    first = before is None
    if last:
        shape = jax.ShapeDtypeStruct((8, 8, 64, 128), jnp.float32)
    else:
        shape = jax.ShapeDtypeStruct((512, 1024), jnp.float32)
    args = (core, own, other, left, col_inv) + (() if first else (before,))
    return pl.pallas_call(
        lambda *refs: pair_kernel(bands, first, last, *refs),
        in_specs=[SCALAR] + [WHOLE] * (len(args) - 1),
        out_specs=WHOLE,
        out_shape=shape,
        scratch_shapes=[
            pltpu.VMEM((bands, 256, 1024), jnp.bfloat16),
            pltpu.VMEM((bands, 8, 1024), jnp.float32),
        ],
        compiler_params=pltpu.CompilerParams(vmem_limit_bytes=24 * 2**20),
    )(*args)


def body(scale, coeffs):
    core = lax.axis_index("core")
    chan = lax.axis_index("chip") * 2 + core
    band = lax.axis_index("band")
    core = core.astype(jnp.int32).reshape(1)
    total = None
    for c, sent in enumerate(turned(core, coeffs)):
        own = lax.all_to_all(sent, "chip", 0, 0, tiled=True)
        other = lax.ppermute(own, "core", [(0, 1), (1, 0)])
        left, col_inv = lefts(core, own)
        total = pairs(core, own, other, left, col_inv, total, c == len(CHUNKS) - 1)
    coded = total.reshape(64, 64, 128).astype(jnp.float16)
    coded = lax.all_to_all(coded, ("band", "chip"), 0, 0, tiled=True)
    coded = coded.astype(jnp.float32)
    value = jnp.where(coded < 0, coded * (-1 / LINEAR), jnp.sqrt(coded * (1 / SQUARE)))
    total = jnp.sum(value, axis=0) * scale
    row = lax.broadcasted_iota(jnp.int32, (64, 128), 0) + chan * 64
    col = lax.broadcasted_iota(jnp.int32, (64, 128), 1) + band * 128
    return jnp.where(row == col, jnp.float32(0.0), total)


def solution(mesh):
    fine = Mesh(mesh.devices.reshape(8, 8, 2), ("band", "chip", "core"))
    scale = W * K / 512

    def whole(coeffs):
        return jax.shard_map(
            lambda x: body(scale, x),
            mesh=fine,
            in_specs=(P(None, None, ("chip", "core"), "band"),),
            out_specs=P(("chip", "core"), "band"),
            check_vma=False,
        )(coeffs)

    return whole
```

time: 329 us -> 81.1 us (0.25)
  waiting for transfers between devices: 180 us -> 19.3 us
  local copies, waits for them, and re-layouts: 58.2 us -> 1.59 us
  other arithmetic: 38.6 us -> 2.81 us
  matrix products: 25.2 us -> 0 us
  blocking collectives: 11.8 us -> 36.1 us
  Pallas kernels: 0 us -> 14.6 us
  between operations: 13.5 us -> 0.06 us
  starting transfers between devices: 0.01 us -> 6.44 us
    all_gather x1 -> x0, waiting for transfers between devices: 180 us -> none  [body(): piece = lax.all_gather(coeffs, 'chan', axis=2, tiled=True)]
    all_gather x1 -> x0, local copies, waits for them, and re-layouts: 45.1 us -> none  [body(): piece = lax.all_gather(coeffs, 'chan', axis=2, tiled=True)]
    reduce_sum x6 -> x1, other arithmetic: 33.8 us -> 0.88 us  [body(): total = jnp.sum(value, axis=0) * scale]
    dot_general x1 -> x0, matrix products: 25.2 us -> none  [body(): jnp.einsum('pkinw,pkjnw->nij', left_side, right_side, preferred_element_t...]
    all_to_all x1, blocking collectives: 11.8 us -> 36.1 us  [body(): own = lax.all_to_all(sent, 'chip', 0, 0, tiled=True)]
    all_to_all x0 -> x1, waiting for transfers between devices: none -> 19.3 us  [body(): coded = lax.all_to_all(coded, ('band', 'chip'), 0, 0, tiled=True)]
    pallas_call x0 -> x3, Pallas kernels: none -> 14.6 us  [the longest x1 8.86 us: pairs(): pl.pallas_call(lambda *refs: pair_kernel(bands, first, last, *refs), in_s...]
    all_to_all x0 -> x1, starting transfers between devices: none -> 6.43 us  [body(): coded = lax.all_to_all(coded, ('band', 'chip'), 0, 0, tiled=True)]
  transfers between devices with their start and end apart: 1 -> 2, of which waited for: 1 -> 1; matrix products, arithmetic and copies ran while one was open for 2% -> 0% of each run, Pallas kernels for 0% -> 6%
where the time goes in v2:
time: 81.1 us; the launch traced here: 80.8 us
  blocking collectives  36.1 us (45%)
  waiting for transfers between devices  19.3 us (24%)
  Pallas kernels  14.6 us (18%)
  starting transfers between devices  6.44 us (8%)
  other arithmetic  2.81 us (3%)
  local copies, waits for them, and re-layouts  1.59 us (2%)
    all_to_all x1, blocking collectives, body(): own = lax.all_to_all(sent, 'chip', 0, 0, tiled=True)  36.1 us
    all_to_all x1, waiting for transfers between devices, body(): coded = lax.all_to_all(coded, ('band', 'chip'), 0, 0, tiled=True)  19.3 us
    pallas_call x1, Pallas kernels, pairs(): pl.pallas_call(lambda *refs: pair_kernel(bands, first, last, *refs), in_s...  8.86 us
    all_to_all x1, starting transfers between devices, body(): coded = lax.all_to_all(coded, ('band', 'chip'), 0, 0, tiled=True)  6.43 us
    pallas_call x1, Pallas kernels, lefts(): pl.pallas_call(left_kernel, in_specs=[SCALAR, WHOLE], out_specs=[WHOLE] *...  4.53 us
  transfers between devices with their start and end apart: 2, of which 1 were waited for; matrix products, arithmetic and copies ran while one was open for 0% of the time, Pallas kernels for 6%

profile of v2, /device:TPU:0, one launch (start us, length us, event | category | flops | bytes accessed | tf_op | source)
XLA Modules:
  0.0 80.8 jit_solution(6308738107027481505)
XLA Ops:
  0.0 0.0 copy-start
  0.0 1.6 %copy-done = bf16[2,8,64,1024]{3,2,1,0:T(8,128)(2,1)S(1)} copy-done((bf16[2,8,64,1024]{3,2,1,0:T(8,128)(2,1)S(1)}, bf16[2,8,64,1024]{3,2,1,0:T(8,128)(2,1)}, u32[]{:S(2)}) %copy-start) | copy-done | bytes 2097176
  1.6 1.2 %shard_map.17 = bf16[8,8,128,128]{3,2,1,0:T(8,128)(2,1)S(1)} custom-call(s32[1]{0:T(128)} %bitcast.core_ref.refs_0_, bf16[2,8,64,1024]{3,2,1,0:T(8,128)(2,1)S(1)} %copy-done), custom_call_target="tpu_custom_call" | custom-call | tf_op jit(solution)/shard_map/pallas_call | solution.py:50
  2.8 36.1 %all_to_all.10.x_ref.refs_1_ = bf16[8,8,128,128]{3,2,1,0:T(8,128)(2,1)S(1)} all-to-all(bf16[8,8,128,128]{3,2,1,0:T(8,128)(2,1)S(1)} %shard_map.17), channel_id=1, replica_groups=mesh['band'=8,'chip'=8,'core'=2] {'chip'}, dimensions={0} | all-to-all | bytes 4194304 | tf_op jit(solution)/shard_map/all_to_all | solution.py:187
  38.9 0.0 collective-permute-start
  38.9 4.5 %shard_map.18 = (bf16[2,8,512,256]{3,2,1,0:T(8,128)(2,1)S(1)}, f32[8,512,128]{2,1,0:T(8,128)S(1)}) custom-call(s32[1]{0:T(128)} %bitcast.core_ref.refs_0_, bf16[8,8,128,128]{3,2,1,0:T(8,128)(2,1)S(1)} %all_to_all.10.x_ref.refs_1_), custom_call_target="tpu_custom_call" | custom-call | tf_op jit(solution)/shard_map/pallas_call | solution.py:92
  43.4 0.0 collective-permute-done.refs_2_
  43.4 8.9 %shard_map.19 = f32[8,8,64,128]{3,2,1,0:T(8,128)S(1)} custom-call(s32[1]{0:T(128)} %bitcast.core_ref.refs_0_, bf16[8,8,128,128]{3,2,1,0:T(8,128)(2,1)S(1)} %all_to_all.10.x_ref.refs_1_, bf16[8,8,128,128]{3,2,1,0:T(8,128)(2,1)S(1)} %collective-permute-done.refs_2_, bf16[2,8,512,256]{3,2,1,0:T(8,128)(2,1)S(1)} %get-tuple-element.7.refs_3_, ...), custom_call_target="tpu_custom_call" | custom-call | tf_op jit(solution)/shard_map/pallas_call | solution.py:167
  52.3 1.2 %convert_element_type.9 = f16[8,8,64,128]{3,2,1,0:T(8,128)(2,1)} convert(f32[8,8,64,128]{3,2,1,0:T(8,128)S(1)} %shard_map.19) | non-fusion elementwise | flops 524288 | bytes 3145728 | tf_op jit(solution)/shard_map/convert_element_type | solution.py:191
  53.5 6.4 %all-to-all-start.1 = ((f16[64,64,128]{2,1,0:T(8,128)(2,1)}), f16[64,64,128]{2,1,0:T(8,128)(2,1)S(1)}, u32[]{:S(2)}, u32[]{:S(2)}) async-start(f16[64,64,128]{2,1,0:T(8,128)(2,1)} %bitcast.1), calls=%async_computation.1 | async-start | bytes 2097152 | tf_op jit(solution)/shard_map/all_to_all | solution.py:192
  60.0 19.3 %all-to-all-done.1 = f16[64,64,128]{2,1,0:T(8,128)(2,1)S(1)} async-done(((f16[64,64,128]{2,1,0:T(8,128)(2,1)}), f16[64,64,128]{2,1,0:T(8,128)(2,1)S(1)}, u32[]{:S(2)}, u32[]{:S(2)}) %all-to-all-start.1) | async-done | bytes 1048608 | tf_op jit(solution)/shard_map/all_to_all | solution.py:192
  79.3 0.9 %fusion.1 = f32[64,128]{1,0:T(8,128)S(1)} fusion(f16[64,64,128]{2,1,0:T(8,128)(2,1)S(1)} %all-to-all-done.1), kind=kLoop, calls=%fused_computation.4 | loop fusion | flops 3137536 | bytes 1081344 | tf_op jit(solution)/shard_map/reduce_sum | solution.py:195
  80.1 0.7 multiply_select_fusion
  (2 shorter events, 0.0 us)
Async XLA Ops:
  0.0 1.6 %copy-start = (bf16[2,8,64,1024]{3,2,1,0:T(8,128)(2,1)S(1)}, bf16[2,8,64,1024]{3,2,1,0:T(8,128)(2,1)}, u32[]{:S(2)}) copy-start(bf16[2,8,64,1024]{3,2,1,0:T(8,128)(2,1)} %x_ref.1) | copy-start | bytes 6291460
  38.9 4.5 %collective-permute-start = (bf16[8,8,128,128]{3,2,1,0:T(8,128)(2,1)S(1)}, bf16[8,8,128,128]{3,2,1,0:T(8,128)(2,1)S(1)}, u32[]{:S(2)}, u32[]{:S(2)}) collective-permute-start(bf16[8,8,128,128]{3,2,1,0:T(8,128)(2,1)S(1)} %all_to_all.10.x_ref.refs_1_), channel_id=1, source_target_pairs={{0,1},{1,0},{2,3},{3,2},{4,5},{5,4},{6,7},{7,6},{8,9},{9,8},{10,11... | collective-permute-start | bytes 6291464 | tf_op jit(solution)/shard_map/ppermute | solution.py:188
  53.5 25.8 %all-to-all-start.1 = ((f16[64,64,128]{2,1,0:T(8,128)(2,1)}), f16[64,64,128]{2,1,0:T(8,128)(2,1)S(1)}, u32[]{:S(2)}, u32[]{:S(2)}) async-start(f16[64,64,128]{2,1,0:T(8,128)(2,1)} %bitcast.1), calls=%async_computation.1 | async-start | bytes 2097152 | tf_op jit(solution)/shard_map/all_to_all | solution.py:192

commit v3 on v0

v3 whole, which is shorter than its diff:
```python
import jax
import jax.numpy as jnp
from jax import lax
from jax.experimental import pallas as pl
from jax.experimental.pallas import tpu as pltpu
from jax.sharding import Mesh, PartitionSpec as P

K = 8
W = 16
EPS = 1e-06
BANDS = 8

LIMIT = 2.0**-11
SQUARE = 2.0**8
LINEAR = 2.0**26

WHOLE = pl.BlockSpec(memory_space=pltpu.VMEM)
SCALAR = pl.BlockSpec(memory_space=pltpu.SMEM)


def swapped(x):
    return jnp.concatenate((x[:, 64:], x[:, :64]), axis=1)


def turn_kernel(core_ref, x_ref, o_ref):
    core = core_ref[0]

    def step(k, carry):
        for t in range(8):
            lanes = slice(t * 128, (t + 1) * 128)
            first = x_ref[core, k, :, lanes]
            second = x_ref[1 - core, k, :, lanes]
            o_ref[t, k] = jnp.concatenate((first, second), axis=0).T
        return carry

    lax.fori_loop(0, K, step, 0)


def turned(core, coeffs):
    return pl.pallas_call(
        turn_kernel,
        in_specs=[SCALAR, WHOLE],
        out_specs=WHOLE,
        out_shape=jax.ShapeDtypeStruct((8, K, 128, 128), jnp.bfloat16),
        compiler_params=pltpu.CompilerParams(vmem_limit_bytes=8 * 2**20),
    )(core, coeffs)


def arrange(side, x_ref, right, row_inv):
    low = lax.broadcasted_iota(jnp.int32, (128, 128), 1) < 64

    def step(m, carry):
        lanes = pl.ds(pl.multiple_of(m * 128, 128), 128)
        for k in range(K):
            a = x_ref[2 * m, k]
            b = x_ref[2 * m + 1, k]
            first = jnp.where(low, a, swapped(b))
            second = jnp.where(low, swapped(a), b)
            at_first = pl.ds(pl.multiple_of(side * 128 + k * W, W), W)
            at_second = pl.ds(pl.multiple_of((1 - side) * 128 + k * W, W), W)
            for n in range(BANDS):
                right[n, at_first, lanes] = first[n * W : (n + 1) * W]
                right[n, at_second, lanes] = second[n * W : (n + 1) * W]
        for n in range(BANDS):
            wide = right[n, :, lanes].astype(jnp.float32)
            power = jnp.sum(wide * wide, axis=0, keepdims=True) + EPS
            row_inv[n : n + 1, lanes] = 1.0 / power
        return carry

    lax.fori_loop(0, 4, step, 0)


def coherence(rows, cols, left, right, row_inv, col_inv):
    total = jnp.zeros((128, 256), jnp.float32)
    for n in range(BANDS):
        lhs = jnp.concatenate((left[0, n, rows, :], left[1, n, rows, :]), axis=0)
        both = jnp.dot(lhs, right[n, :, cols], preferred_element_type=jnp.float32)
        re = both[:128]
        im = both[128:]
        ci = col_inv[n, rows, :]
        ci = jnp.concatenate((ci, ci), axis=1)
        total += (re * re + im * im) * row_inv[n : n + 1, cols] * ci
    return total


def own_kernel(core_ref, x_ref, left, col_inv, o_ref, right, row_inv):
    arrange(core_ref[0], x_ref, right, row_inv)

    def turn(m, carry):
        lanes = pl.ds(pl.multiple_of(m * 128, 128), 128)
        columns = row_inv[:, lanes].T
        for n in range(BANDS):
            block = right[n, :, lanes].T
            left[0, n, lanes, :] = block
            left[1, n, lanes, 0:128] = block[:, 128:]
            left[1, n, lanes, 128:256] = -block[:, :128]
            col_inv[n, lanes, :] = jnp.broadcast_to(columns[:, n : n + 1], (128, 128))
        return carry

    lax.fori_loop(0, 4, turn, 0)

    def tile(i, carry):
        rows = pl.ds(pl.multiple_of(i * 128, 128), 128)
        for j in range(2):
            cols = slice(j * 256, (j + 1) * 256)
            o_ref[rows, cols] = coherence(rows, cols, left, right, row_inv, col_inv)
        return carry

    lax.fori_loop(0, 4, tile, 0)


ARRANGED = [
    pltpu.VMEM((BANDS, 256, 512), jnp.bfloat16),
    pltpu.VMEM((BANDS, 512), jnp.float32),
]


def own_pairs(core, x):
    return pl.pallas_call(
        own_kernel,
        in_specs=[SCALAR, WHOLE],
        out_specs=[WHOLE] * 3,
        out_shape=[
            jax.ShapeDtypeStruct((2, BANDS, 512, 256), jnp.bfloat16),
            jax.ShapeDtypeStruct((BANDS, 512, 128), jnp.float32),
            jax.ShapeDtypeStruct((512, 512), jnp.float32),
        ],
        scratch_shapes=ARRANGED,
        compiler_params=pltpu.CompilerParams(vmem_limit_bytes=16 * 2**20),
    )(core, x)


def other_kernel(core_ref, x_ref, left, col_inv, own_ref, o_ref, right, row_inv):
    arrange(1 - core_ref[0], x_ref, right, row_inv)
    first_core = core_ref[0] == 0
    low = lax.broadcasted_iota(jnp.int32, (128, 128), 1) < 64

    def tile(i, carry):
        rows = pl.ds(pl.multiple_of(i * 128, 128), 128)
        for j in range(2):
            cols = slice(j * 256, (j + 1) * 256)
            total = coherence(rows, cols, left, right, row_inv, col_inv)
            for half in range(2):
                m = 2 * j + half
                own = own_ref[rows, m * 128 : (m + 1) * 128]
                other = total[:, half * 128 : (half + 1) * 128]
                zero = jnp.where(first_core, own, other)
                one = jnp.where(first_core, other, own)
                for g in range(2):
                    if g == 0:
                        sums = jnp.where(low, zero, swapped(one))
                    else:
                        sums = jnp.where(low, swapped(zero), one)
                    coded = jnp.where(sums >= LIMIT, sums * sums * SQUARE, sums * -LINEAR)
                    for h in range(2):
                        o_ref[2 * m + g, 2 * i + h] = coded[h * 64 : (h + 1) * 64]
        return carry

    lax.fori_loop(0, 4, tile, 0)


def other_pairs(core, x, left, col_inv, own):
    return pl.pallas_call(
        other_kernel,
        in_specs=[SCALAR] + [WHOLE] * 4,
        out_specs=WHOLE,
        out_shape=jax.ShapeDtypeStruct((8, 8, 64, 128), jnp.float32),
        scratch_shapes=ARRANGED,
        compiler_params=pltpu.CompilerParams(vmem_limit_bytes=16 * 2**20),
    )(core, x, left, col_inv, own)


def body(scale, coeffs):
    core = lax.axis_index("core")
    chan = lax.axis_index("chip") * 2 + core
    band = lax.axis_index("band")
    side = core.astype(jnp.int32).reshape(1)
    own = lax.all_to_all(turned(side, coeffs), "chip", 0, 0, tiled=True)
    other = lax.ppermute(own, "core", [(0, 1), (1, 0)])
    left, col_inv, sums = own_pairs(side, own)
    coded = other_pairs(side, other, left, col_inv, sums)
    coded = coded.reshape(64, 64, 128).astype(jnp.float16)
    coded = lax.all_to_all(coded, ("band", "chip"), 0, 0, tiled=True).astype(jnp.float32)
    value = jnp.where(coded < 0, coded * (-1 / LINEAR), jnp.sqrt(coded * (1 / SQUARE)))
    row = lax.broadcasted_iota(jnp.int32, (64, 64, 128), 1) + chan * 64
    col = lax.broadcasted_iota(jnp.int32, (64, 64, 128), 2) + band * 128
    return jnp.sum(jnp.where(row == col, jnp.float32(0.0), value * scale), axis=0)


def solution(mesh):
    fine = Mesh(mesh.devices.reshape(8, 8, 2), ("band", "chip", "core"))
    scale = W * K / 512

    def whole(coeffs):
        return jax.shard_map(
            lambda x: body(scale, x),
            mesh=fine,
            in_specs=(P(None, None, ("chip", "core"), "band"),),
            out_specs=P(("chip", "core"), "band"),
            check_vma=False,
        )(coeffs)

    return whole
```

time: 329 us -> 78.8 us (0.24)
  waiting for transfers between devices: 180 us -> 19.3 us
  local copies, waits for them, and re-layouts: 58.2 us -> 1.59 us
  other arithmetic: 38.6 us -> 2.88 us
  matrix products: 25.2 us -> 0 us
  blocking collectives: 11.8 us -> 36.1 us
  between operations: 13.5 us -> 0.07 us
  Pallas kernels: 0 us -> 12.3 us
  starting transfers between devices: 0.01 us -> 6.44 us
    all_gather x1 -> x0, waiting for transfers between devices: 180 us -> none  [body(): piece = lax.all_gather(coeffs, 'chan', axis=2, tiled=True)]
    all_gather x1 -> x0, local copies, waits for them, and re-layouts: 45.1 us -> none  [body(): piece = lax.all_gather(coeffs, 'chan', axis=2, tiled=True)]
    reduce_sum x6 -> x1, other arithmetic: 33.8 us -> 1.64 us  [body(): jnp.sum(jnp.where(row == col, jnp.float32(0.0), value * scale), axis=0)]
    dot_general x1 -> x0, matrix products: 25.2 us -> none  [body(): jnp.einsum('pkinw,pkjnw->nij', left_side, right_side, preferred_element_t...]
    all_to_all x1, blocking collectives: 11.8 us -> 36.1 us  [body(): own = lax.all_to_all(turned(side, coeffs), 'chip', 0, 0, tiled=True)]
    all_to_all x0 -> x1, waiting for transfers between devices: none -> 19.3 us  [body(): lax.all_to_all(coded, ('band', 'chip'), 0, 0, tiled=True)]
    pallas_call x0 -> x3, Pallas kernels: none -> 12.3 us  [the longest x1 6.07 us: own_pairs(): pl.pallas_call(own_kernel, in_specs=[SCALAR, WHOLE], out_specs=[WHOLE] *...]
    all_to_all x0 -> x1, starting transfers between devices: none -> 6.43 us  [body(): lax.all_to_all(coded, ('band', 'chip'), 0, 0, tiled=True)]
  transfers between devices with their start and end apart: 1 -> 2, of which waited for: 1 -> 1; matrix products, arithmetic and copies ran while one was open for 2% -> 0% of each run, Pallas kernels for 0% -> 8%
where the time goes in v3:
time: 78.8 us; the launch traced here: 78.6 us
  blocking collectives  36.1 us (46%)
  waiting for transfers between devices  19.3 us (24%)
  Pallas kernels  12.3 us (16%)
  starting transfers between devices  6.44 us (8%)
  other arithmetic  2.88 us (4%)
  local copies, waits for them, and re-layouts  1.59 us (2%)
    all_to_all x1, blocking collectives, body(): own = lax.all_to_all(turned(side, coeffs), 'chip', 0, 0, tiled=True)  36.1 us
    all_to_all x1, waiting for transfers between devices, body(): lax.all_to_all(coded, ('band', 'chip'), 0, 0, tiled=True)  19.3 us
    all_to_all x1, starting transfers between devices, body(): lax.all_to_all(coded, ('band', 'chip'), 0, 0, tiled=True)  6.43 us
    pallas_call x1, Pallas kernels, own_pairs(): pl.pallas_call(own_kernel, in_specs=[SCALAR, WHOLE], out_specs=[WHOLE] *...  6.07 us
    pallas_call x1, Pallas kernels, other_pairs(): pl.pallas_call(other_kernel, in_specs=[SCALAR] + [WHOLE] * 4, out_specs=W...  5.23 us
    reduce_sum x1, other arithmetic, body(): jnp.sum(jnp.where(row == col, jnp.float32(0.0), value * scale), axis=0)  1.64 us
    unnamed x2, local copies, waits for them, and re-layouts  1.59 us
  transfers between devices with their start and end apart: 2, of which 1 were waited for; matrix products, arithmetic and copies ran while one was open for 0% of the time, Pallas kernels for 8%

profile of v3, /device:TPU:0, one launch (start us, length us, event | category | flops | bytes accessed | tf_op | source)
XLA Modules:
  0.0 78.6 jit_solution(6446615199540430256)
XLA Ops:
  0.0 0.0 copy-start
  0.0 1.6 %copy-done = bf16[2,8,64,1024]{3,2,1,0:T(8,128)(2,1)S(1)} copy-done((bf16[2,8,64,1024]{3,2,1,0:T(8,128)(2,1)S(1)}, bf16[2,8,64,1024]{3,2,1,0:T(8,128)(2,1)}, u32[]{:S(2)}) %copy-start) | copy-done | bytes 2097176
  1.6 1.0 %shard_map.17 = bf16[8,8,128,128]{3,2,1,0:T(8,128)(2,1)S(1)} custom-call(s32[1]{0:T(128)} %bitcast.core_ref, bf16[2,8,64,1024]{3,2,1,0:T(8,128)(2,1)S(1)} %copy-done), custom_call_target="tpu_custom_call" | custom-call | tf_op jit(solution)/shard_map/pallas_call | solution.py:40
  2.6 36.1 %all_to_all.10.x_ref = bf16[8,8,128,128]{3,2,1,0:T(8,128)(2,1)S(1)} all-to-all(bf16[8,8,128,128]{3,2,1,0:T(8,128)(2,1)S(1)} %shard_map.17), channel_id=1, replica_groups=mesh['band'=8,'chip'=8,'core'=2] {'chip'}, dimensions={0} | all-to-all | bytes 4194304 | tf_op jit(solution)/shard_map/all_to_all | solution.py:178
  38.6 0.0 collective-permute-start
  38.6 6.1 %shard_map.18 = (bf16[2,8,512,256]{3,2,1,0:T(8,128)(2,1)S(1)}, f32[8,512,128]{2,1,0:T(8,128)S(1)}, f32[512,512]{1,0:T(8,128)S(1)}) custom-call(s32[1]{0:T(128)} %bitcast.core_ref, bf16[8,8,128,128]{3,2,1,0:T(8,128)(2,1)S(1)} %all_to_all.10.x_ref), custom_call_target="tpu_custom_call" | custom-call | tf_op jit(solution)/shard_map/pallas_call | solution.py:119
  44.7 0.0 collective-permute-done.x_ref
  44.7 5.2 %shard_map.19 = f32[8,8,64,128]{3,2,1,0:T(8,128)S(1)} custom-call(s32[1]{0:T(128)} %bitcast.core_ref, bf16[8,8,128,128]{3,2,1,0:T(8,128)(2,1)S(1)} %collective-permute-done.x_ref, bf16[2,8,512,256]{3,2,1,0:T(8,128)(2,1)S(1)} %get-tuple-element.8.left, f32[8,512,128]{2,1,0:T(8,128)S(1)} %get-tuple-element.9.col_inv, f32[512,512]{1,0:T(8,128)S(1)} %get-tuple-element.10.own_ref), custom_call_target="tpu_custom_call" | custom-call | tf_op jit(solution)/shard_map/pallas_call | solution.py:163
  50.0 1.2 %convert_element_type.9 = f16[8,8,64,128]{3,2,1,0:T(8,128)(2,1)} convert(f32[8,8,64,128]{3,2,1,0:T(8,128)S(1)} %shard_map.19) | non-fusion elementwise | flops 524288 | bytes 3145728 | tf_op jit(solution)/shard_map/convert_element_type | solution.py:182
  51.2 6.4 %all-to-all-start.1 = ((f16[64,64,128]{2,1,0:T(8,128)(2,1)}), f16[64,64,128]{2,1,0:T(8,128)(2,1)S(1)}, u32[]{:S(2)}, u32[]{:S(2)}) async-start(f16[64,64,128]{2,1,0:T(8,128)(2,1)} %bitcast.1), calls=%async_computation.1 | async-start | bytes 2097152 | tf_op jit(solution)/shard_map/all_to_all | solution.py:183
  57.7 19.3 %all-to-all-done.1 = f16[64,64,128]{2,1,0:T(8,128)(2,1)S(1)} async-done(((f16[64,64,128]{2,1,0:T(8,128)(2,1)}), f16[64,64,128]{2,1,0:T(8,128)(2,1)S(1)}, u32[]{:S(2)}, u32[]{:S(2)}) %all-to-all-start.1) | async-done | bytes 1048608 | tf_op jit(solution)/shard_map/all_to_all | solution.py:183
  76.9 1.6 %fusion.3 = f32[64,128]{1,0:T(8,128)} fusion(f16[64,64,128]{2,1,0:T(8,128)(2,1)S(1)} %all-to-all-done.1, s32[128]{0:T(128)S(1)} %iota_add_fusion, s32[64]{0:T(128)S(1)} %iota_add_fusion.1), kind=kLoop, calls=%fused_computation.6 | loop fusion | flops 4710400 | bytes 1082112 | tf_op jit(solution)/shard_map/reduce_sum | solution.py:187
  (2 shorter events, 0.0 us)
Async XLA Ops:
  0.0 1.6 %copy-start = (bf16[2,8,64,1024]{3,2,1,0:T(8,128)(2,1)S(1)}, bf16[2,8,64,1024]{3,2,1,0:T(8,128)(2,1)}, u32[]{:S(2)}) copy-start(bf16[2,8,64,1024]{3,2,1,0:T(8,128)(2,1)} %x_ref.1) | copy-start | bytes 6291460
  38.6 6.1 %collective-permute-start = (bf16[8,8,128,128]{3,2,1,0:T(8,128)(2,1)S(1)}, bf16[8,8,128,128]{3,2,1,0:T(8,128)(2,1)S(1)}, u32[]{:S(2)}, u32[]{:S(2)}) collective-permute-start(bf16[8,8,128,128]{3,2,1,0:T(8,128)(2,1)S(1)} %all_to_all.10.x_ref), channel_id=1, source_target_pairs={{0,1},{1,0},{2,3},{3,2},{4,5},{5,4},{6,7},{7,6},{8,9},{9,8},{10,11... | collective-permute-start | bytes 6291464 | tf_op jit(solution)/shard_map/ppermute | solution.py:179
  51.2 25.7 %all-to-all-start.1 = ((f16[64,64,128]{2,1,0:T(8,128)(2,1)}), f16[64,64,128]{2,1,0:T(8,128)(2,1)S(1)}, u32[]{:S(2)}, u32[]{:S(2)}) async-start(f16[64,64,128]{2,1,0:T(8,128)(2,1)} %bitcast.1), calls=%async_computation.1 | async-start | bytes 2097152 | tf_op jit(solution)/shard_map/all_to_all | solution.py:183

commit v4 on v3

v4 whole, which is shorter than its diff:
```python
import jax
import jax.numpy as jnp
from jax import lax
from jax.experimental import pallas as pl
from jax.experimental.pallas import tpu as pltpu
from jax.sharding import Mesh, PartitionSpec as P

K = 8
W = 16
EPS = 1e-06
BANDS = 8

LIMIT = 2.0**-11
SQUARE = 2.0**8
LINEAR = 2.0**26

WHOLE = pl.BlockSpec(memory_space=pltpu.VMEM)
SCALAR = pl.BlockSpec(memory_space=pltpu.SMEM)


def swapped(x):
    return jnp.concatenate((x[:, 64:], x[:, :64]), axis=1)


def turn_kernel(core_ref, x_hbm, o_ref, x_ref, sems):
    core = core_ref[0]

    def fetch(k):
        return pltpu.make_async_copy(x_hbm.at[:, k], x_ref.at[:, k], sems.at[k])

    for k in range(K):
        fetch(k).start()

    def step(k, carry):
        fetch(k).wait()
        for t in range(8):
            lanes = slice(t * 128, (t + 1) * 128)
            first = x_ref[core, k, :, lanes]
            second = x_ref[1 - core, k, :, lanes]
            o_ref[t, k] = jnp.concatenate((first, second), axis=0).T
        return carry

    lax.fori_loop(0, K, step, 0)


def turned(core, coeffs):
    return pl.pallas_call(
        turn_kernel,
        in_specs=[SCALAR, pl.BlockSpec(memory_space=pltpu.HBM)],
        out_specs=WHOLE,
        out_shape=jax.ShapeDtypeStruct((8, K, 128, 128), jnp.bfloat16),
        scratch_shapes=[
            pltpu.VMEM(coeffs.shape, jnp.bfloat16),
            pltpu.SemaphoreType.DMA((K,)),
        ],
        compiler_params=pltpu.CompilerParams(vmem_limit_bytes=8 * 2**20),
    )(core, pltpu.with_memory_space_constraint(coeffs, pltpu.HBM))


def arrange(side, x_ref, right, row_inv):
    low = lax.broadcasted_iota(jnp.int32, (128, 128), 1) < 64

    def step(m, carry):
        power = [jnp.zeros((8, 128), jnp.float32)] * BANDS
        for k in range(K):
            a = x_ref[2 * m, k]
            b = x_ref[2 * m + 1, k]
            for part, block in (
                (side, jnp.where(low, a, swapped(b))),
                (1 - side, jnp.where(low, swapped(a), b)),
            ):
                for n in range(BANDS):
                    rows = block[n * W : (n + 1) * W]
                    right[n, m, part * K + k] = rows
                    wide = rows.astype(jnp.float32)
                    wide = wide * wide
                    power[n] += wide[:8] + wide[8:]
        for n in range(BANDS):
            total = jnp.sum(power[n], axis=0, keepdims=True) + EPS
            row_inv[m, n : n + 1, :] = 1.0 / total
        return carry

    lax.fori_loop(0, 4, step, 0)


def coherence(rows, j, left, right, row_inv, col_inv):
    total = jnp.zeros((128, 256), jnp.float32)
    for n in range(BANDS):
        re = left[0, n, rows, :]
        im = left[1, n, rows, :]
        for_re = jnp.concatenate((re, im), axis=1)
        for_im = jnp.concatenate((im, left[2, n, rows, :]), axis=1)
        lhs = jnp.concatenate((for_re, for_im), axis=0)
        rhs = jnp.concatenate(
            (right[n, 2 * j].reshape(256, 128), right[n, 2 * j + 1].reshape(256, 128)), axis=1
        )
        both = jnp.dot(lhs, rhs, preferred_element_type=jnp.float32)
        re = both[:128]
        im = both[128:]
        ri = jnp.concatenate((row_inv[2 * j, n : n + 1, :], row_inv[2 * j + 1, n : n + 1, :]), axis=1)
        ci = col_inv[n, rows, :]
        ci = jnp.concatenate((ci, ci), axis=1)
        total += (re * re + im * im) * ri * ci
    return total


def own_kernel(core_ref, x_ref, left, col_inv, o_ref, right, row_inv):
    arrange(core_ref[0], x_ref, right, row_inv)

    def tile(i, carry):
        rows = pl.ds(pl.multiple_of(i * 128, 128), 128)
        columns = row_inv[i].T
        for n in range(BANDS):
            block = right[n, i].reshape(256, 128).T
            left[0, n, rows, :] = block[:, :128]
            left[1, n, rows, :] = block[:, 128:]
            left[2, n, rows, :] = -block[:, :128]
            col_inv[n, rows, :] = jnp.broadcast_to(columns[:, n : n + 1], (128, 128))
        row = lax.broadcasted_iota(jnp.int32, (128, 256), 0) + i * 128
        col = lax.broadcasted_iota(jnp.int32, (128, 256), 1)
        for j in range(2):
            cols = slice(j * 256, (j + 1) * 256)
            total = coherence(rows, j, left, right, row_inv, col_inv)
            o_ref[rows, cols] = jnp.where(row == col + j * 256, 0.0, total)
        return carry

    lax.fori_loop(0, 4, tile, 0)


ARRANGED = [
    pltpu.VMEM((BANDS, 4, 2 * K, W, 128), jnp.bfloat16),
    pltpu.VMEM((4, BANDS, 128), jnp.float32),
]


def own_pairs(core, x):
    return pl.pallas_call(
        own_kernel,
        in_specs=[SCALAR, WHOLE],
        out_specs=[WHOLE] * 3,
        out_shape=[
            jax.ShapeDtypeStruct((3, BANDS, 512, 128), jnp.bfloat16),
            jax.ShapeDtypeStruct((BANDS, 512, 128), jnp.float32),
            jax.ShapeDtypeStruct((512, 512), jnp.float32),
        ],
        scratch_shapes=ARRANGED,
        compiler_params=pltpu.CompilerParams(vmem_limit_bytes=16 * 2**20),
    )(core, x)


def other_kernel(core_ref, x_ref, left, col_inv, own_ref, o_ref, right, row_inv):
    arrange(1 - core_ref[0], x_ref, right, row_inv)
    first_core = core_ref[0] == 0
    low = lax.broadcasted_iota(jnp.int32, (128, 128), 1) < 64

    def tile(i, carry):
        rows = pl.ds(pl.multiple_of(i * 128, 128), 128)
        for j in range(2):
            total = coherence(rows, j, left, right, row_inv, col_inv)
            for half in range(2):
                m = 2 * j + half
                own = own_ref[rows, m * 128 : (m + 1) * 128]
                other = total[:, half * 128 : (half + 1) * 128]
                zero = jnp.where(first_core, own, other)
                one = jnp.where(first_core, other, own)
                for g in range(2):
                    if g == 0:
                        sums = jnp.where(low, zero, swapped(one))
                    else:
                        sums = jnp.where(low, swapped(zero), one)
                    coded = jnp.where(sums >= LIMIT, sums * sums * SQUARE, sums * -LINEAR)
                    for h in range(2):
                        o_ref[2 * i + h, 2 * m + g] = coded[h * 64 : (h + 1) * 64]
        return carry

    lax.fori_loop(0, 4, tile, 0)


def other_pairs(core, x, left, col_inv, own):
    return pl.pallas_call(
        other_kernel,
        in_specs=[SCALAR] + [WHOLE] * 4,
        out_specs=WHOLE,
        out_shape=jax.ShapeDtypeStruct((8, 8, 64, 128), jnp.float32),
        scratch_shapes=ARRANGED,
        compiler_params=pltpu.CompilerParams(vmem_limit_bytes=16 * 2**20),
    )(core, x, left, col_inv, own)


def body(scale, coeffs):
    core = lax.axis_index("core")
    side = core.astype(jnp.int32).reshape(1)
    own = lax.all_to_all(turned(side, coeffs), "chip", 0, 0, tiled=True)
    other = lax.ppermute(own, "core", [(0, 1), (1, 0)])
    left, col_inv, sums = own_pairs(side, own)
    coded = other_pairs(side, other, left, col_inv, sums)
    coded = coded.reshape(64, 64, 128).astype(jnp.float16)
    coded = lax.all_to_all(coded, ("chip", "band"), 0, 0, tiled=True).astype(jnp.float32)
    square = coded * lax.rsqrt(coded) * (scale / SQUARE**0.5)
    return jnp.sum(jnp.where(coded > 0, square, coded * (-scale / LINEAR)), axis=0)


def solution(mesh):
    fine = Mesh(mesh.devices.reshape(8, 8, 2), ("band", "chip", "core"))
    scale = W * K / 512

    def whole(coeffs):
        return jax.shard_map(
            lambda x: body(scale, x),
            mesh=fine,
            in_specs=(P(None, None, ("chip", "core"), "band"),),
            out_specs=P(("chip", "core"), "band"),
            check_vma=False,
        )(coeffs)

    return whole
```

time: 78.8 us -> 73.9 us (0.938)
  blocking collectives: 36.1 us -> 60.5 us
  waiting for transfers between devices: 19.3 us -> 0.01 us
  starting transfers between devices: 6.44 us -> 0.01 us
  local copies, waits for them, and re-layouts: 1.59 us -> 0 us
  other arithmetic: 2.88 us -> 1.41 us
    all_to_all x0 -> x1, blocking collectives: none -> 24.4 us  [body(): lax.all_to_all(coded, ('chip', 'band'), 0, 0, tiled=True)]
    all_to_all x1 -> x0, waiting for transfers between devices: 19.3 us -> none  [body(): lax.all_to_all(coded, ('band', 'chip'), 0, 0, tiled=True)]
    all_to_all x1 -> x0, starting transfers between devices: 6.43 us -> none  [body(): lax.all_to_all(coded, ('band', 'chip'), 0, 0, tiled=True)]
    unnamed x2 -> x0, local copies, waits for them, and re-layouts: 1.59 us -> none
    pallas_call x1, Pallas kernels: 6.07 us -> 4.88 us  [own_pairs(): pl.pallas_call(own_kernel, in_specs=[SCALAR, WHOLE], out_specs=[WHOLE] *...]
    pallas_call x1, Pallas kernels: 0.99 us -> 2.02 us  [turned(): pl.pallas_call(turn_kernel, in_specs=[SCALAR, pl.BlockSpec(memory_space=p...]
    convert_element_type x1, other arithmetic: 1.22 us -> 0.25 us  [body(): coded = coded.reshape(64, 64, 128).astype(jnp.float16)]
  transfers between devices with their start and end apart: 2 -> 1, of which waited for: 1 -> 0; matrix products, arithmetic and copies ran while one was open for 0% -> 0% of each run, Pallas kernels for 8% -> 7%
where the time goes in v4:
time: 73.9 us; the launch traced here: 73.7 us
  blocking collectives  60.5 us (82%)
  Pallas kernels  11.8 us (16%)
  other arithmetic  1.41 us (2%)
    all_to_all x1, blocking collectives, body(): own = lax.all_to_all(turned(side, coeffs), 'chip', 0, 0, tiled=True)  36.1 us
    all_to_all x1, blocking collectives, body(): lax.all_to_all(coded, ('chip', 'band'), 0, 0, tiled=True)  24.4 us
    pallas_call x1, Pallas kernels, other_pairs(): pl.pallas_call(other_kernel, in_specs=[SCALAR] + [WHOLE] * 4, out_specs=W...  4.91 us
    pallas_call x1, Pallas kernels, own_pairs(): pl.pallas_call(own_kernel, in_specs=[SCALAR, WHOLE], out_specs=[WHOLE] *...  4.88 us
    pallas_call x1, Pallas kernels, turned(): pl.pallas_call(turn_kernel, in_specs=[SCALAR, pl.BlockSpec(memory_space=p...  2.02 us
  transfers between devices with their start and end apart: 1, of which 0 were waited for; matrix products, arithmetic and copies ran while one was open for 0% of the time, Pallas kernels for 7%

profile of v4, /device:TPU:0, one launch (start us, length us, event | category | flops | bytes accessed | tf_op | source)
XLA Modules:
  0.0 73.7 jit_solution(11249416163328882569)
XLA Ops:
  0.0 2.0 %shard_map.17 = bf16[8,8,128,128]{3,2,1,0:T(8,128)(2,1)S(1)} custom-call(s32[1]{0:T(128)} %bitcast.core_ref, bf16[2,8,64,1024]{3,2,1,0:T(8,128)(2,1)} %x_hbm.1), custom_call_target="tpu_custom_call" | custom-call | tf_op jit(solution)/shard_map/pallas_call | solution.py:47
  2.0 36.1 %all_to_all.10.x_ref = bf16[8,8,128,128]{3,2,1,0:T(8,128)(2,1)S(1)} all-to-all(bf16[8,8,128,128]{3,2,1,0:T(8,128)(2,1)S(1)} %shard_map.17), channel_id=1, replica_groups=mesh['band'=8,'chip'=8,'core'=2] {'chip'}, dimensions={0} | all-to-all | bytes 4194304 | tf_op jit(solution)/shard_map/all_to_all | solution.py:193
  38.1 0.0 collective-permute-start
  38.1 4.9 %shard_map.18 = (bf16[3,8,512,128]{3,2,1,0:T(8,128)(2,1)S(1)}, f32[8,512,128]{2,1,0:T(8,128)S(1)}, f32[512,512]{1,0:T(8,128)S(1)}) custom-call(s32[1]{0:T(128)} %bitcast.core_ref, bf16[8,8,128,128]{3,2,1,0:T(8,128)(2,1)S(1)} %all_to_all.10.x_ref), custom_call_target="tpu_custom_call" | custom-call | tf_op jit(solution)/shard_map/pallas_call | solution.py:137
  43.0 0.0 collective-permute-done.x_ref
  43.0 4.9 %shard_map.19 = f32[8,8,64,128]{3,2,1,0:T(8,128)S(1)} custom-call(s32[1]{0:T(128)} %bitcast.core_ref, bf16[8,8,128,128]{3,2,1,0:T(8,128)(2,1)S(1)} %collective-permute-done.x_ref, bf16[3,8,512,128]{3,2,1,0:T(8,128)(2,1)S(1)} %get-tuple-element.8.left, f32[8,512,128]{2,1,0:T(8,128)S(1)} %get-tuple-element.9.col_inv, f32[512,512]{1,0:T(8,128)S(1)} %get-tuple-element.10.own_ref), custom_call_target="tpu_custom_call" | custom-call | tf_op jit(solution)/shard_map/pallas_call | solution.py:180
  47.9 0.2 convert_element_type.9
  48.2 24.4 %all_to_all.11 = f16[64,64,128]{2,1,0:T(8,128)(2,1)S(1)} all-to-all(f16[64,64,128]{2,1,0:T(8,128)(2,1)S(1)} %bitcast.2), channel_id=1, replica_groups=mesh['band'=8,'chip'=8,'core'=2] {'chip','band'}, dimensions={0} | all-to-all | bytes 2097152 | tf_op jit(solution)/shard_map/all_to_all | solution.py:198
  72.6 1.2 %fusion.2 = f32[64,128]{1,0:T(8,128)} fusion(f16[64,64,128]{2,1,0:T(8,128)(2,1)S(1)} %all_to_all.11), kind=kLoop, calls=%fused_computation.6 | loop fusion | flops 3661824 | bytes 1081344 | tf_op jit(solution)/shard_map/reduce_sum | solution.py:200
Async XLA Ops:
  38.1 4.9 %collective-permute-start = (bf16[8,8,128,128]{3,2,1,0:T(8,128)(2,1)S(1)}, bf16[8,8,128,128]{3,2,1,0:T(8,128)(2,1)S(1)}, u32[]{:S(2)}, u32[]{:S(2)}) collective-permute-start(bf16[8,8,128,128]{3,2,1,0:T(8,128)(2,1)S(1)} %all_to_all.10.x_ref), channel_id=1, source_target_pairs={{0,1},{1,0},{2,3},{3,2},{4,5},{5,4},{6,7},{7,6},{8,9},{9,8},{10,11... | collective-permute-start | bytes 6291464 | tf_op jit(solution)/shard_map/ppermute | solution.py:194

commit v5 on v0

v5 whole, which is shorter than its diff:
```python
import jax
import jax.numpy as jnp
from jax import lax
from jax.experimental import pallas as pl
from jax.experimental.pallas import tpu as pltpu
from jax.sharding import Mesh, PartitionSpec as P


K = 8
W = 16
EPS = 1e-06
BANDS = 8

STEPS = ((0, 0), (0, 1), (0, 3), (0, 2), (1, 0), (1, 1), (1, 3), (1, 2))

LIMIT = 2.0**-11
SQUARE = 2.0**8
LINEAR = 2.0**26

WHOLE = pl.BlockSpec(memory_space=pltpu.VMEM)
SCALAR = pl.BlockSpec(memory_space=pltpu.SMEM)
PIECE = (K, BANDS * W, 128)
ARRANGED = (BANDS, 2, 2 * K + 1, W, 128)


def chip_at(chip, step, sign):
    half = (chip >> 2) ^ step[0]
    return (half << 2) + ((chip + sign * step[1]) & 3)


def swapped(x):
    return jnp.concatenate((x[:, 64:], x[:, :64]), axis=1)


def call(kernel, mib, out, scratch=(), products=0):
    many = isinstance(out, list)

    def run(place, *args, first=WHOLE):
        return pl.pallas_call(
            kernel,
            in_specs=[SCALAR, first] + [WHOLE] * (len(args) - 1),
            out_specs=[WHOLE] * len(out) if many else WHOLE,
            out_shape=out,
            scratch_shapes=list(scratch),
            cost_estimate=pl.CostEstimate(
                flops=products * BANDS * 2 * 256**3, bytes_accessed=2**20, transcendentals=0
            ),
            compiler_params=pltpu.CompilerParams(vmem_limit_bytes=mib * 2**20),
        )(place, *args)

    return run


def turn_kernel(place, x_hbm, *refs):
    outs = refs[: len(STEPS)]
    x_ref, sems = refs[len(STEPS) :]
    core = place[0]
    chip = place[1]

    def fetch(k):
        return pltpu.make_async_copy(x_hbm.at[:, k], x_ref.at[:, k], sems.at[k])

    for k in range(K):
        fetch(k).start()

    def step(k, carry):
        fetch(k).wait()
        for o_ref, go in zip(outs, STEPS):
            lanes = pl.ds(pl.multiple_of(chip_at(chip, go, 1) * 128, 128), 128)
            first = x_ref[core, k, :, lanes]
            second = x_ref[1 - core, k, :, lanes]
            o_ref[k] = jnp.concatenate((first, second), axis=0).T
        return carry

    lax.fori_loop(0, K, step, 0)


def turned(place, coeffs):
    piece = jax.ShapeDtypeStruct(PIECE, jnp.bfloat16)
    run = call(
        turn_kernel,
        8,
        [piece] * len(STEPS),
        (pltpu.VMEM(coeffs.shape, jnp.bfloat16), pltpu.SemaphoreType.DMA((K,))),
    )
    coeffs = pltpu.with_memory_space_constraint(coeffs, pltpu.HBM)
    return run(place, coeffs, first=pl.BlockSpec(memory_space=pltpu.HBM))


def arrange_kernel(place, x0, x1, x2, x3, right):
    side = place[0]
    low = lax.broadcasted_iota(jnp.int32, (128, 128), 1) < 64
    row = lax.broadcasted_iota(jnp.int32, (W, 128), 0)
    for m, (a_ref, b_ref) in enumerate(((x0, x1), (x2, x3))):

        def step(k, power):
            power = list(power)
            a = a_ref[k]
            b = b_ref[k]
            for part, block in (
                (side, jnp.where(low, a, swapped(b))),
                (1 - side, jnp.where(low, swapped(a), b)),
            ):
                for n in range(BANDS):
                    rows = block[n * W : (n + 1) * W]
                    right[n, m, part * K + k] = rows
                    wide = rows.astype(jnp.float32)
                    wide = wide * wide
                    power[n] += wide[:8] + wide[8:]
            return tuple(power)

        power = (jnp.zeros((8, 128), jnp.float32),) * BANDS
        for k in range(K):
            power = step(k, power)
        for n in range(BANDS):
            inv = 1.0 / (jnp.sum(power[n], axis=0, keepdims=True) + EPS)
            high = inv.astype(jnp.bfloat16).astype(jnp.float32)
            middle = (inv - high).astype(jnp.bfloat16).astype(jnp.float32)
            rest = inv - high - middle
            parts = jnp.where(row == 0, high, jnp.where(row == 1, middle, jnp.where(row == 2, rest, 0.0)))
            right[n, m, 2 * K] = parts.astype(jnp.bfloat16)


arranged = call(arrange_kernel, 8, jax.ShapeDtypeStruct(ARRANGED, jnp.bfloat16), products=1)


def inverse(right, n, m):
    parts = right[n, m, 2 * K].astype(jnp.float32)
    return jnp.sum(parts, axis=0, keepdims=True)


def columns(right, n, m):
    return right[n, m, 0 : 2 * K].reshape(256, 128)


def turn_left(i, right, left, col_inv):
    rows = pl.ds(pl.multiple_of(i * 128, 128), 128)
    inv = jnp.concatenate([inverse(right, n, i) for n in range(BANDS)], axis=0).T
    for n in range(BANDS):
        block = columns(right, n, i).T
        left[0, n, rows, :] = block[:, :128]
        left[1, n, rows, :] = block[:, 128:]
        left[2, n, rows, :] = -block[:, :128]
        col_inv[n, rows, :] = jnp.broadcast_to(inv[:, n : n + 1], (128, 128))


def coherence(i, left, col_inv, right):
    rows = pl.ds(pl.multiple_of(i * 128, 128), 128)
    total = jnp.zeros((128, 256), jnp.float32)
    for n in range(BANDS):
        re = left[0, n, rows, :]
        im = left[1, n, rows, :]
        for_re = jnp.concatenate((re, im), axis=1)
        for_im = jnp.concatenate((im, left[2, n, rows, :]), axis=1)
        lhs = jnp.concatenate((for_re, for_im), axis=0)
        rhs = jnp.concatenate((columns(right, n, 0), columns(right, n, 1)), axis=1)
        both = jnp.dot(lhs, rhs, preferred_element_type=jnp.float32)
        re = both[:128]
        im = both[128:]
        ri = jnp.concatenate((inverse(right, n, 0), inverse(right, n, 1)), axis=1)
        ci = col_inv[n, rows, :]
        ci = jnp.concatenate((ci, ci), axis=1)
        total += (re * re + im * im) * ri * ci
    return total


def no_diagonal(i, total):
    row = lax.broadcasted_iota(jnp.int32, (128, 256), 0) + i * 128
    col = lax.broadcasted_iota(jnp.int32, (128, 256), 1)
    return jnp.where(row == col, 0.0, total)


LEFT = jax.ShapeDtypeStruct((3, BANDS, 256, 128), jnp.bfloat16)
COL_INV = jax.ShapeDtypeStruct((BANDS, 256, 128), jnp.float32)
BLOCK = jax.ShapeDtypeStruct((256, 256), jnp.float32)


def near_own_kernel(place, right, left, col_inv, o_ref):
    def tile(i, carry):
        rows = pl.ds(pl.multiple_of(i * 128, 128), 128)
        turn_left(i, right, left, col_inv)
        o_ref[rows, :] = no_diagonal(i, coherence(i, left, col_inv, right))
        return carry

    lax.fori_loop(0, 2, tile, 0)


def near_other_kernel(place, right, left, col_inv, o_ref):
    def tile(i, carry):
        rows = pl.ds(pl.multiple_of(i * 128, 128), 128)
        o_ref[rows, :] = coherence(i, left, col_inv, right)
        return carry

    lax.fori_loop(0, 2, tile, 0)


def far_own_kernel(place, right0, right1, left1, col_inv1, o10, o11):
    def tile(i, carry):
        rows = pl.ds(pl.multiple_of(i * 128, 128), 128)
        turn_left(i, right1, left1, col_inv1)
        o10[rows, :] = coherence(i, left1, col_inv1, right0)
        o11[rows, :] = no_diagonal(i, coherence(i, left1, col_inv1, right1))
        return carry

    lax.fori_loop(0, 2, tile, 0)


def far_other_kernel(
    place, right0, right1, left0, col_inv0, left1, col_inv1, a00, a10, a11, b00, o_ref
):
    first_core = place[0] == 0
    chip = place[1]
    low = lax.broadcasted_iota(jnp.int32, (128, 128), 1) < 64

    def put(i, a, b, own_ref, total):
        rows = pl.ds(pl.multiple_of(i * 128, 128), 128)
        for m in range(2):
            lanes = slice(m * 128, (m + 1) * 128)
            own = own_ref[lanes, rows].T if a < b else own_ref[rows, lanes]
            other = total[:, lanes]
            zero = jnp.where(first_core, own, other)
            one = jnp.where(first_core, other, own)
            for g in range(2):
                if g == 0:
                    sums = jnp.where(low, zero, swapped(one))
                else:
                    sums = jnp.where(low, swapped(zero), one)
                coded = jnp.where(sums >= LIMIT, sums * sums * SQUARE, sums * -LINEAR)
                to = chip_at(chip, STEPS[4 * b + 2 * m + g], -1)
                for h in range(2):
                    even = chip_at(chip, STEPS[4 * a + h], -1)
                    odd = chip_at(chip, STEPS[4 * a + 2 + h], -1)
                    o_ref[jnp.where(i == 0, even, odd), to] = coded[h * 64 : (h + 1) * 64]

    def tile(i, carry):
        rows = pl.ds(pl.multiple_of(i * 128, 128), 128)
        put(i, 0, 0, a00, b00[rows, :])
        put(i, 0, 1, a10, coherence(i, left0, col_inv0, right1))
        put(i, 1, 0, a10, coherence(i, left1, col_inv1, right0))
        put(i, 1, 1, a11, coherence(i, left1, col_inv1, right1))
        return carry

    lax.fori_loop(0, 2, tile, 0)


near_own = call(near_own_kernel, 8, [LEFT, COL_INV, BLOCK], products=2)
near_other = call(near_other_kernel, 8, BLOCK, products=2)
far_own = call(far_own_kernel, 8, [LEFT, COL_INV, BLOCK, BLOCK], products=4)
far_other = call(
    far_other_kernel, 8, jax.ShapeDtypeStruct((8, 8, 64, 128), jnp.float32), products=6
)


def body(scale, coeffs):
    core = lax.axis_index("core")
    chip = lax.axis_index("chip")
    place = jnp.stack((core, chip)).astype(jnp.int32)
    pieces = list(turned(place, coeffs))
    for p in range(1, len(STEPS)):
        pairs = [(c, chip_at(c, STEPS[p], 1)) for c in range(8)]
        pieces[p] = lax.ppermute(pieces[p], "chip", pairs)
    swap = [(0, 1), (1, 0)]
    own0 = arranged(place, *pieces[:4])
    other0 = lax.ppermute(own0, "core", swap)
    left0, col_inv0, a00 = near_own(place, own0)
    b00 = near_other(place, other0, left0, col_inv0)
    own1 = arranged(place, *pieces[4:])
    other1 = lax.ppermute(own1, "core", swap)
    left1, col_inv1, a10, a11 = far_own(place, own0, own1)
    coded = far_other(
        place, other0, other1, left0, col_inv0, left1, col_inv1, a00, a10, a11, b00
    )
    coded = coded.reshape(64, 64, 128).astype(jnp.float16)
    coded = lax.all_to_all(coded, ("chip", "band"), 0, 0, tiled=True).astype(jnp.float32)
    square = coded * lax.rsqrt(coded) * (scale / SQUARE**0.5)
    return jnp.sum(jnp.where(coded > 0, square, coded * (-scale / LINEAR)), axis=0)


def solution(mesh):
    fine = Mesh(mesh.devices.reshape(8, 8, 2), ("band", "chip", "core"))
    scale = W * K / 512

    def step(coeffs):
        return body(scale, coeffs)

    return jax.shard_map(
        step,
        mesh=fine,
        in_specs=(P(None, None, ("chip", "core"), "band"),),
        out_specs=P(("chip", "core"), "band"),
        check_vma=False,
    )
```

time: 329 us -> 74.9 us (0.23)
  waiting for transfers between devices: 180 us -> 8.28 us
  local copies, waits for them, and re-layouts: 58.2 us -> 0 us
  other arithmetic: 38.6 us -> 1.48 us
  matrix products: 25.2 us -> 0 us
  starting transfers between devices: 0.01 us -> 23.9 us
  blocking collectives: 11.8 us -> 27 us
  Pallas kernels: 0 us -> 14 us
  between operations: 13.5 us -> 0.12 us
    all_gather x1 -> x0, waiting for transfers between devices: 180 us -> none  [body(): piece = lax.all_gather(coeffs, 'chan', axis=2, tiled=True)]
    all_gather x1 -> x0, local copies, waits for them, and re-layouts: 45.1 us -> none  [body(): piece = lax.all_gather(coeffs, 'chan', axis=2, tiled=True)]
    reduce_sum x6 -> x1, other arithmetic: 33.8 us -> 1.16 us  [body(): jnp.sum(jnp.where(coded > 0, square, coded * (-scale / LINEAR)), axis=0)]
    dot_general x1 -> x0, matrix products: 25.2 us -> none  [body(): jnp.einsum('pkinw,pkjnw->nij', left_side, right_side, preferred_element_t...]
    ppermute x0 -> x9, starting transfers between devices: none -> 23.9 us  [the longest x7 23.8 us: body(): pieces[p] = lax.ppermute(pieces[p], 'chip', pairs)]
    all_to_all x1, blocking collectives: 11.8 us -> 27 us  [body(): lax.all_to_all(coded, ('chip', 'band'), 0, 0, tiled=True)]
    pallas_call x0 -> x7, Pallas kernels: none -> 14 us  [run(): pl.pallas_call(kernel, in_specs=[SCALAR, first] + [WHOLE] * (len(args) -...]
    ppermute x0 -> x9, waiting for transfers between devices: none -> 8.28 us  [the longest x7 8.27 us: body(): pieces[p] = lax.ppermute(pieces[p], 'chip', pairs)]
  transfers between devices with their start and end apart: 1 -> 9, of which waited for: 1 -> 3; matrix products, arithmetic and copies ran while one was open for 2% -> 0% of each run, Pallas kernels for 0% -> 10%
where the time goes in v5:
time: 74.9 us; the launch traced here: 74.7 us
  blocking collectives  27 us (36%)
  starting transfers between devices  23.9 us (32%)
  Pallas kernels  14 us (19%)
  waiting for transfers between devices  8.28 us (11%)
  other arithmetic  1.48 us (2%)
    all_to_all x1, blocking collectives, body(): lax.all_to_all(coded, ('chip', 'band'), 0, 0, tiled=True)  27 us
    ppermute x7, starting transfers between devices, body(): pieces[p] = lax.ppermute(pieces[p], 'chip', pairs)  23.8 us
    pallas_call x7, Pallas kernels, run(): pl.pallas_call(kernel, in_specs=[SCALAR, first] + [WHOLE] * (len(args) -...  14 us
    ppermute x7, waiting for transfers between devices, body(): pieces[p] = lax.ppermute(pieces[p], 'chip', pairs)  8.27 us
  transfers between devices with their start and end apart: 9, of which 3 were waited for; matrix products, arithmetic and copies ran while one was open for 0% of the time, Pallas kernels for 10%

profile of v5, /device:TPU:0, one launch (start us, length us, event | category | flops | bytes accessed | tf_op | source)
XLA Modules:
  0.0 74.7 jit_solution(5788321191058592678)
XLA Ops:
  0.0 0.1 pad_add_fusion.place
  0.1 2.6 %shard_map.17 = (bf16[8,128,128]{2,1,0:T(8,128)(2,1)S(1)}, bf16[8,128,128]{2,1,0:T(8,128)(2,1)S(1)}, bf16[8,128,128]{2,1,0:T(8,128)(2,1)S(1)}, bf16[8,128,128]{2...) custom-call(s32[2]{0:T(128)S(1)} %pad_add_fusion.place, ...), custom_call_target="tpu_custom_call" | custom-call | bytes 1048576 | tf_op jit(solution)/shard_map/pallas_call | solution.py:39
  2.7 2.1 %collective-permute-start = (bf16[8,128,128]{2,1,0:T(8,128)(2,1)S(1)}, bf16[8,128,128]{2,1,0:T(8,128)(2,1)S(1)}, u32[]{:S(2)}, u32[]{:S(2)}) collective-permute-start(bf16[8,128,128]{2,1,0:T(8,128)(2,1)S(1)} %get-tuple-element.21), channel_id=1, source_target_pairs={{0,2},{2,4},{4,6},{6,0},{8,10},{10,12},{12,14},{14,8},{1,3},{3,5},... | collective-permute-start | bytes 786440 | tf_op jit(solution)/shard_map/ppermute | solution.py:261
  4.8 2.2 %collective-permute-start.1 = (bf16[8,128,128]{2,1,0:T(8,128)(2,1)S(1)}, bf16[8,128,128]{2,1,0:T(8,128)(2,1)S(1)}, u32[]{:S(2)}, u32[]{:S(2)}) collective-permute-start(bf16[8,128,128]{2,1,0:T(8,128)(2,1)S(1)} %get-tuple-element.22), channel_id=1, source_target_pairs={{0,6},{2,0},{4,2},{6,4},{8,14},{10,8},{12,10},{14,12},{1,7},{3,1},... | collective-permute-start | bytes 786440 | tf_op jit(solution)/shard_map/ppermute | solution.py:261
  7.0 1.8 %collective-permute-start.2 = (bf16[8,128,128]{2,1,0:T(8,128)(2,1)S(1)}, bf16[8,128,128]{2,1,0:T(8,128)(2,1)S(1)}, u32[]{:S(2)}, u32[]{:S(2)}) collective-permute-start(bf16[8,128,128]{2,1,0:T(8,128)(2,1)S(1)} %get-tuple-element.23), channel_id=1, source_target_pairs={{0,4},{2,6},{4,0},{6,2},{8,12},{10,14},{12,8},{14,10},{1,5},{3,7},... | collective-permute-start | bytes 786440 | tf_op jit(solution)/shard_map/ppermute | solution.py:261
  8.7 3.0 %collective-permute-start.4 = (bf16[8,128,128]{2,1,0:T(8,128)(2,1)S(1)}, bf16[8,128,128]{2,1,0:T(8,128)(2,1)S(1)}, u32[]{:S(2)}, u32[]{:S(2)}) collective-permute-start(bf16[8,128,128]{2,1,0:T(8,128)(2,1)S(1)} %get-tuple-element.24), channel_id=1, source_target_pairs={{0,8},{2,10},{4,12},{6,14},{8,0},{10,2},{12,4},{14,6},{1,9},{3,11}... | collective-permute-start | bytes 786440 | tf_op jit(solution)/shard_map/ppermute | solution.py:261
  11.8 1.0 %collective-permute-start.5 = (bf16[8,128,128]{2,1,0:T(8,128)(2,1)S(1)}, bf16[8,128,128]{2,1,0:T(8,128)(2,1)S(1)}, u32[]{:S(2)}, u32[]{:S(2)}) collective-permute-start(bf16[8,128,128]{2,1,0:T(8,128)(2,1)S(1)} %get-tuple-element.25), channel_id=1, source_target_pairs={{0,10},{2,12},{4,14},{6,8},{8,2},{10,4},{12,6},{14,0},{1,11},{3,13... | collective-permute-start | bytes 786440 | tf_op jit(solution)/shard_map/ppermute | solution.py:261
  12.7 0.5 collective-permute-done.x1
  13.2 5.3 %collective-permute-start.6 = (bf16[8,128,128]{2,1,0:T(8,128)(2,1)S(1)}, bf16[8,128,128]{2,1,0:T(8,128)(2,1)S(1)}, u32[]{:S(2)}, u32[]{:S(2)}) collective-permute-start(bf16[8,128,128]{2,1,0:T(8,128)(2,1)S(1)} %get-tuple-element.26), channel_id=1, source_target_pairs={{0,14},{2,8},{4,10},{6,12},{8,6},{10,0},{12,2},{14,4},{1,15},{3,9}... | collective-permute-start | bytes 786440 | tf_op jit(solution)/shard_map/ppermute | solution.py:261
  18.5 8.4 %collective-permute-start.7 = (bf16[8,128,128]{2,1,0:T(8,128)(2,1)S(1)}, bf16[8,128,128]{2,1,0:T(8,128)(2,1)S(1)}, u32[]{:S(2)}, u32[]{:S(2)}) collective-permute-start(bf16[8,128,128]{2,1,0:T(8,128)(2,1)S(1)} %get-tuple-element.27), channel_id=1, source_target_pairs={{0,12},{2,14},{4,8},{6,10},{8,4},{10,6},{12,0},{14,2},{1,13},{3,15... | collective-permute-start | bytes 786440 | tf_op jit(solution)/shard_map/ppermute | solution.py:261
  26.9 1.0 %shard_map.18.right.right0 = bf16[8,2,17,16,128]{4,3,2,1,0:T(8,128)(2,1)S(1)} custom-call(s32[2]{0:T(128)S(1)} %pad_add_fusion.place, bf16[8,128,128]{2,1,0:T(8,128)(2,1)S(1)} %get-tuple-element.20.x0, bf16[8,128,128]{2,1,0:T(8,128)(2,1)S(1)} %collective-permute-done.x1, bf16[8,128,128]{2,1,0:T(8,128)(2,1)S(1)} %collective-permute-done.1.x2, ...), custom_call_target="tpu_custom_call" | custom-call | flops 268435456 | bytes 1048576 | tf_op jit(solution)/shard_map/pallas_call | solution.py:39
  27.9 0.1 collective-permute-start.3
  28.0 0.0 collective-permute-done.4.x0
  28.0 3.4 %collective-permute-done.6.x2 = bf16[8,128,128]{2,1,0:T(8,128)(2,1)S(1)} collective-permute-done((bf16[8,128,128]{2,1,0:T(8,128)(2,1)S(1)}, bf16[8,128,128]{2,1,0:T(8,128)(2,1)S(1)}, u32[]{:S(2)}, u32[]{:S(2)}) %collective-permute-start.6) | collective-permute-done | bytes 262176 | tf_op jit(solution)/shard_map/ppermute | solution.py:261
  31.4 4.4 %collective-permute-done.7.x3 = bf16[8,128,128]{2,1,0:T(8,128)(2,1)S(1)} collective-permute-done((bf16[8,128,128]{2,1,0:T(8,128)(2,1)S(1)}, bf16[8,128,128]{2,1,0:T(8,128)(2,1)S(1)}, u32[]{:S(2)}, u32[]{:S(2)}) %collective-permute-start.7) | collective-permute-done | bytes 262176 | tf_op jit(solution)/shard_map/ppermute | solution.py:261
  35.8 1.0 %shard_map.19.right1 = bf16[8,2,17,16,128]{4,3,2,1,0:T(8,128)(2,1)S(1)} custom-call(s32[2]{0:T(128)S(1)} %pad_add_fusion.place, bf16[8,128,128]{2,1,0:T(8,128)(2,1)S(1)} %collective-permute-done.4.x0, bf16[8,128,128]{2,1,0:T(8,128)(2,1)S(1)} %collective-permute-done.5.x1, bf16[8,128,128]{2,1,0:T(8,128)(2,1)S(1)} %collective-permute-done.6.x2, ...), custom_call_target="tpu_custom_call" | custom-call | flops 268435456 | bytes 1048576 | tf_op jit(solution)/shard_map/pallas_call | solution.py:39
  36.8 0.1 collective-permute-start.8
  36.9 1.7 %shard_map.20 = (bf16[3,8,256,128]{3,2,1,0:T(8,128)(2,1)S(1)}, f32[8,256,128]{2,1,0:T(8,128)S(1)}, f32[256,256]{1,0:T(8,128)S(1)}) custom-call(s32[2]{0:T(128)S(1)} %pad_add_fusion.place, bf16[8,2,17,16,128]{4,3,2,1,0:T(8,128)(2,1)S(1)} %shard_map.18.right.right0), custom_call_target="tpu_custom_call" | custom-call | flops 536870912 | bytes 1048576 | tf_op jit(solution)/shard_map/pallas_call | solution.py:39
  38.6 2.5 %shard_map.21 = (bf16[3,8,256,128]{3,2,1,0:T(8,128)(2,1)S(1)}, f32[8,256,128]{2,1,0:T(8,128)S(1)}, f32[256,256]{1,0:T(8,128)S(1)}, f32[256,256]{1,0:T(8,128)S(1)}) custom-call(s32[2]{0:T(128)S(1)} %pad_add_fusion.place, bf16[8,2,17,16,128]{4,3,2,1,0:T(8,128)(2,1)S(1)} %shard_map.18.right.right0, bf16[8,2,17,16,128]{4,3,2,1,0:T(8,128)(2,1)S(1)} %shard_map.19.right1), custom_call_target="tpu_custom_call" | custom-call | flops 1073741824 | bytes 1048576 | tf_op jit(solution)/shard_map/pallas_call | solution.py:39
  41.2 1.5 %shard_map.22.b00 = f32[256,256]{1,0:T(8,128)S(1)} custom-call(s32[2]{0:T(128)S(1)} %pad_add_fusion.place, bf16[8,2,17,16,128]{4,3,2,1,0:T(8,128)(2,1)S(1)} %collective-permute-done.3.right.right0, bf16[3,8,256,128]{3,2,1,0:T(8,128)(2,1)S(1)} %get-tuple-element.28.left.left0, f32[8,256,128]{2,1,0:T(8,128)S(1)} %get-tuple-element.29.col_inv.col_inv0), custom_call_target="tpu_custom_call" | custom-call | flops 536870912 | bytes 1048576 | tf_op jit(solution)/shard_map/pallas_call | solution.py:39
  42.7 3.7 %shard_map.23 = f32[8,8,64,128]{3,2,1,0:T(8,128)S(1)} custom-call(s32[2]{0:T(128)S(1)} %pad_add_fusion.place, bf16[8,2,17,16,128]{4,3,2,1,0:T(8,128)(2,1)S(1)} %collective-permute-done.3.right.right0, bf16[8,2,17,16,128]{4,3,2,1,0:T(8,128)(2,1)S(1)} %collective-permute-done.8.right1, bf16[3,8,256,128]{3,2,1,0:T(8,128)(2,1)S(1)} %get-tuple-element.28.left.left0, ...), custom_call_target="tpu_custom_call" | custom-call | flops 1610612736 | bytes 1048576 | tf_op jit(solution)/shard_map/pallas_call | solution.py:39
  46.4 0.2 convert_element_type.9
  46.6 27.0 %all_to_all.5 = f16[64,64,128]{2,1,0:T(8,128)(2,1)S(1)} all-to-all(f16[64,64,128]{2,1,0:T(8,128)(2,1)S(1)} %bitcast.3), channel_id=1, replica_groups=mesh['band'=8,'chip'=8,'core'=2] {'chip','band'}, dimensions={0} | all-to-all | bytes 2097152 | tf_op jit(solution)/shard_map/all_to_all | solution.py:274
  73.6 1.2 %fusion.2 = f32[64,128]{1,0:T(8,128)} fusion(f16[64,64,128]{2,1,0:T(8,128)(2,1)S(1)} %all_to_all.5), kind=kLoop, calls=%fused_computation.6 | loop fusion | flops 3661824 | bytes 1081344 | tf_op jit(solution)/shard_map/reduce_sum | solution.py:276
  (5 shorter events, 0.0 us)
Async XLA Ops:
  2.7 10.5 %collective-permute-start = (bf16[8,128,128]{2,1,0:T(8,128)(2,1)S(1)}, bf16[8,128,128]{2,1,0:T(8,128)(2,1)S(1)}, u32[]{:S(2)}, u32[]{:S(2)}) collective-permute-start(bf16[8,128,128]{2,1,0:T(8,128)(2,1)S(1)} %get-tuple-element.21), channel_id=1, source_target_pairs={{0,2},{2,4},{4,6},{6,0},{8,10},{10,12},{12,14},{14,8},{1,3},{3,5},... | collective-permute-start | bytes 786440 | tf_op jit(solution)/shard_map/ppermute | solution.py:261
  4.8 13.8 %collective-permute-start.1 = (bf16[8,128,128]{2,1,0:T(8,128)(2,1)S(1)}, bf16[8,128,128]{2,1,0:T(8,128)(2,1)S(1)}, u32[]{:S(2)}, u32[]{:S(2)}) collective-permute-start(bf16[8,128,128]{2,1,0:T(8,128)(2,1)S(1)} %get-tuple-element.22), channel_id=1, source_target_pairs={{0,6},{2,0},{4,2},{6,4},{8,14},{10,8},{12,10},{14,12},{1,7},{3,1},... | collective-permute-start | bytes 786440 | tf_op jit(solution)/shard_map/ppermute | solution.py:261
  7.0 19.9 %collective-permute-start.2 = (bf16[8,128,128]{2,1,0:T(8,128)(2,1)S(1)}, bf16[8,128,128]{2,1,0:T(8,128)(2,1)S(1)}, u32[]{:S(2)}, u32[]{:S(2)}) collective-permute-start(bf16[8,128,128]{2,1,0:T(8,128)(2,1)S(1)} %get-tuple-element.23), channel_id=1, source_target_pairs={{0,4},{2,6},{4,0},{6,2},{8,12},{10,14},{12,8},{14,10},{1,5},{3,7},... | collective-permute-start | bytes 786440 | tf_op jit(solution)/shard_map/ppermute | solution.py:261
  8.7 19.2 %collective-permute-start.4 = (bf16[8,128,128]{2,1,0:T(8,128)(2,1)S(1)}, bf16[8,128,128]{2,1,0:T(8,128)(2,1)S(1)}, u32[]{:S(2)}, u32[]{:S(2)}) collective-permute-start(bf16[8,128,128]{2,1,0:T(8,128)(2,1)S(1)} %get-tuple-element.24), channel_id=1, source_target_pairs={{0,8},{2,10},{4,12},{6,14},{8,0},{10,2},{12,4},{14,6},{1,9},{3,11}... | collective-permute-start | bytes 786440 | tf_op jit(solution)/shard_map/ppermute | solution.py:261
  11.8 16.2 %collective-permute-start.5 = (bf16[8,128,128]{2,1,0:T(8,128)(2,1)S(1)}, bf16[8,128,128]{2,1,0:T(8,128)(2,1)S(1)}, u32[]{:S(2)}, u32[]{:S(2)}) collective-permute-start(bf16[8,128,128]{2,1,0:T(8,128)(2,1)S(1)} %get-tuple-element.25), channel_id=1, source_target_pairs={{0,10},{2,12},{4,14},{6,8},{8,2},{10,4},{12,6},{14,0},{1,11},{3,13... | collective-permute-start | bytes 786440 | tf_op jit(solution)/shard_map/ppermute | solution.py:261
  13.2 18.2 %collective-permute-start.6 = (bf16[8,128,128]{2,1,0:T(8,128)(2,1)S(1)}, bf16[8,128,128]{2,1,0:T(8,128)(2,1)S(1)}, u32[]{:S(2)}, u32[]{:S(2)}) collective-permute-start(bf16[8,128,128]{2,1,0:T(8,128)(2,1)S(1)} %get-tuple-element.26), channel_id=1, source_target_pairs={{0,14},{2,8},{4,10},{6,12},{8,6},{10,0},{12,2},{14,4},{1,15},{3,9}... | collective-permute-start | bytes 786440 | tf_op jit(solution)/shard_map/ppermute | solution.py:261
  18.5 17.3 %collective-permute-start.7 = (bf16[8,128,128]{2,1,0:T(8,128)(2,1)S(1)}, bf16[8,128,128]{2,1,0:T(8,128)(2,1)S(1)}, u32[]{:S(2)}, u32[]{:S(2)}) collective-permute-start(bf16[8,128,128]{2,1,0:T(8,128)(2,1)S(1)} %get-tuple-element.27), channel_id=1, source_target_pairs={{0,12},{2,14},{4,8},{6,10},{8,4},{10,6},{12,0},{14,2},{1,13},{3,15... | collective-permute-start | bytes 786440 | tf_op jit(solution)/shard_map/ppermute | solution.py:261
  27.9 13.3 %collective-permute-start.3 = (bf16[8,2,17,16,128]{4,3,2,1,0:T(8,128)(2,1)S(1)}, bf16[8,2,17,16,128]{4,3,2,1,0:T(8,128)(2,1)S(1)}, u32[]{:S(2)}, u32[]{:S(2)}) collective-permute-start(bf16[8,2,17,16,128]{4,3,2,1,0:T(8,128)(2,1)S(1)} %shard_map.18.right.right0), channel_id=1, source_target_pairs={{0,1},{1,0},{2,3},{3,2},{4,5},{5,4},{6,7},{7,6},{8,9},{9,8},{10,11... | collective-permute-start | bytes 3342344 | tf_op jit(solution)/shard_map/ppermute | solution.py:264
  36.8 5.9 %collective-permute-start.8 = (bf16[8,2,17,16,128]{4,3,2,1,0:T(8,128)(2,1)S(1)}, bf16[8,2,17,16,128]{4,3,2,1,0:T(8,128)(2,1)S(1)}, u32[]{:S(2)}, u32[]{:S(2)}) collective-permute-start(bf16[8,2,17,16,128]{4,3,2,1,0:T(8,128)(2,1)S(1)} %shard_map.19.right1), channel_id=1, source_target_pairs={{0,1},{1,0},{2,3},{3,2},{4,5},{5,4},{6,7},{7,6},{8,9},{9,8},{10,11... | collective-permute-start | bytes 3342344 | tf_op jit(solution)/shard_map/ppermute | solution.py:268

commit v6 on v5

--- a/solution.py
+++ b/solution.py
@@ -12,6 +12,8 @@
 BANDS = 8
 
 STEPS = ((0, 0), (0, 1), (0, 3), (0, 2), (1, 0), (1, 1), (1, 3), (1, 2))
+ORDER = (1, 2, 4, 5, 3, 6, 7)
+SPLIT = 3
 
 LIMIT = 2.0**-11
 SQUARE = 2.0**8
@@ -51,39 +53,42 @@
     return run
 
 
-def turn_kernel(place, x_hbm, *refs):
-    outs = refs[: len(STEPS)]
-    x_ref, sems = refs[len(STEPS) :]
+def turn_kernel(steps, place, x_hbm, *refs):
+    outs = refs[: len(steps)]
+    x_ref, sems = refs[len(steps) :]
     core = place[0]
     chip = place[1]
 
-    def fetch(k):
-        return pltpu.make_async_copy(x_hbm.at[:, k], x_ref.at[:, k], sems.at[k])
-
-    for k in range(K):
-        fetch(k).start()
-
-    def step(k, carry):
-        fetch(k).wait()
-        for o_ref, go in zip(outs, STEPS):
-            lanes = pl.ds(pl.multiple_of(chip_at(chip, go, 1) * 128, 128), 128)
-            first = x_ref[core, k, :, lanes]
-            second = x_ref[1 - core, k, :, lanes]
-            o_ref[k] = jnp.concatenate((first, second), axis=0).T
-        return carry
-
-    lax.fori_loop(0, K, step, 0)
-
-
-def turned(place, coeffs):
-    piece = jax.ShapeDtypeStruct(PIECE, jnp.bfloat16)
+    def fetch(p):
+        lanes = pl.ds(pl.multiple_of(chip_at(chip, steps[p], 1) * 128, 128), 128)
+        return pltpu.make_async_copy(x_hbm.at[:, :, :, lanes], x_ref.at[p], sems.at[p])
+
+    for p in range(len(steps)):
+        fetch(p).start()
+    for p in range(len(steps)):
+        fetch(p).wait()
+
+    def step(h, carry):
+        for k in range(K // 2):
+            for p, o_ref in enumerate(outs):
+                first = x_ref[p, core, h * (K // 2) + k]
+                second = x_ref[p, 1 - core, h * (K // 2) + k]
+                o_ref[h * (K // 2) + k] = jnp.concatenate((first, second), axis=0).T
+        return carry
+
+    lax.fori_loop(0, 2, step, 0)
+
+
+def turned(place, coeffs, steps):
     run = call(
-        turn_kernel,
+        lambda *refs: turn_kernel(steps, *refs),
         8,
-        [piece] * len(STEPS),
-        (pltpu.VMEM(coeffs.shape, jnp.bfloat16), pltpu.SemaphoreType.DMA((K,))),
+        [jax.ShapeDtypeStruct(PIECE, jnp.bfloat16)] * len(steps),
+        (
+            pltpu.VMEM((len(steps), 2, K, coeffs.shape[2], 128), jnp.bfloat16),
+            pltpu.SemaphoreType.DMA((len(steps),)),
+        ),
     )
-    coeffs = pltpu.with_memory_space_constraint(coeffs, pltpu.HBM)
     return run(place, coeffs, first=pl.BlockSpec(memory_space=pltpu.HBM))
 
 
@@ -255,7 +260,11 @@
     core = lax.axis_index("core")
     chip = lax.axis_index("chip")
     place = jnp.stack((core, chip)).astype(jnp.int32)
-    pieces = list(turned(place, coeffs))
+    coeffs = pltpu.with_memory_space_constraint(coeffs, pltpu.HBM)
+    pieces = [None] * len(STEPS)
+    for some in (ORDER[:SPLIT], ORDER[SPLIT:] + (0,)):
+        for p, piece in zip(some, turned(place, coeffs, [STEPS[p] for p in some])):
+            pieces[p] = piece
     for p in range(1, len(STEPS)):
         pairs = [(c, chip_at(c, STEPS[p], 1)) for c in range(8)]
         pieces[p] = lax.ppermute(pieces[p], "chip", pairs)

time: 74.9 us -> 77.6 us (1.036)
  starting transfers between devices: 23.9 us -> 19.7 us
  waiting for transfers between devices: 8.28 us -> 12.2 us
  Pallas kernels: 14 us -> 15.7 us
  blocking collectives: 27 us -> 28.2 us
    ppermute x7, starting transfers between devices: 23.8 us -> 19.5 us  [body(): pieces[p] = lax.ppermute(pieces[p], 'chip', pairs)]
    ppermute x7, waiting for transfers between devices: 8.27 us -> 12.2 us  [body(): pieces[p] = lax.ppermute(pieces[p], 'chip', pairs)]
    pallas_call x7 -> x8, Pallas kernels: 14 us -> 15.7 us  [run(): pl.pallas_call(kernel, in_specs=[SCALAR, first] + [WHOLE] * (len(args) -...]
    all_to_all x1, blocking collectives: 27 us -> 28.2 us  [body(): lax.all_to_all(coded, ('chip', 'band'), 0, 0, tiled=True)]
  transfers between devices with their start and end apart: 9 -> 9, of which waited for: 3 -> 3; matrix products, arithmetic and copies ran while one was open for 0% -> 0% of each run, Pallas kernels for 10% -> 13%
where the time goes in v6:
time: 77.6 us; the launch traced here: 77.4 us
  blocking collectives  28.2 us (36%)
  starting transfers between devices  19.7 us (25%)
  Pallas kernels  15.7 us (20%)
  waiting for transfers between devices  12.2 us (16%)
  other arithmetic  1.48 us (2%)
    all_to_all x1, blocking collectives, body(): lax.all_to_all(coded, ('chip', 'band'), 0, 0, tiled=True)  28.2 us
    ppermute x7, starting transfers between devices, body(): pieces[p] = lax.ppermute(pieces[p], 'chip', pairs)  19.5 us
    pallas_call x8, Pallas kernels, run(): pl.pallas_call(kernel, in_specs=[SCALAR, first] + [WHOLE] * (len(args) -...  15.7 us
    ppermute x7, waiting for transfers between devices, body(): pieces[p] = lax.ppermute(pieces[p], 'chip', pairs)  12.2 us
  transfers between devices with their start and end apart: 9, of which 3 were waited for; matrix products, arithmetic and copies ran while one was open for 0% of the time, Pallas kernels for 13%

profile of v6, /device:TPU:0, one launch (start us, length us, event | category | flops | bytes accessed | tf_op | source)
XLA Modules:
  0.0 77.4 jit_solution(9820430828994338710)
XLA Ops:
  0.0 0.1 pad_add_fusion.refs_0_.place
  0.1 2.3 %shard_map.17 = (bf16[8,128,128]{2,1,0:T(8,128)(2,1)S(1)}, bf16[8,128,128]{2,1,0:T(8,128)(2,1)S(1)}, bf16[8,128,128]{2,1,0:T(8,128)(2,1)S(1)}, bf16[8,128,128]{2,1,0:T(8,128)(2,1)S(1)}, bf16[8,128,128]{2,1,0:T(8,128)(2,1)S(1)}) custom-call(s32[2]{0:T(128)S(1)} %pad_add_fusion.refs_0_.place, bf16[2,8,64,1024]{3,2,1,0:T(8,128)(2,1)} %refs_1_.3), custom_call_target="tpu_custom_call" | custom-call | bytes 1048576 | tf_op jit(solution)/shard_map/pallas_call | solution.py:41
  2.4 4.1 %collective-permute-start.2 = (bf16[8,128,128]{2,1,0:T(8,128)(2,1)S(1)}, bf16[8,128,128]{2,1,0:T(8,128)(2,1)S(1)}, u32[]{:S(2)}, u32[]{:S(2)}) collective-permute-start(bf16[8,128,128]{2,1,0:T(8,128)(2,1)S(1)} %get-tuple-element.23), channel_id=1, source_target_pairs={{0,4},{2,6},{4,0},{6,2},{8,12},{10,14},{12,8},{14,10},{1,5},{3,7},... | collective-permute-start | bytes 786440 | tf_op jit(solution)/shard_map/ppermute | solution.py:270
  6.5 2.0 %shard_map.18 = (bf16[8,128,128]{2,1,0:T(8,128)(2,1)S(1)}, bf16[8,128,128]{2,1,0:T(8,128)(2,1)S(1)}, bf16[8,128,128]{2,1,0:T(8,128)(2,1)S(1)}) custom-call(s32[2]{0:T(128)S(1)} %pad_add_fusion.refs_0_.place, bf16[2,8,64,1024]{3,2,1,0:T(8,128)(2,1)} %refs_1_.3), custom_call_target="tpu_custom_call" | custom-call | bytes 1048576 | tf_op jit(solution)/shard_map/pallas_call | solution.py:41
  8.5 1.1 %collective-permute-start = (bf16[8,128,128]{2,1,0:T(8,128)(2,1)S(1)}, bf16[8,128,128]{2,1,0:T(8,128)(2,1)S(1)}, u32[]{:S(2)}, u32[]{:S(2)}) collective-permute-start(bf16[8,128,128]{2,1,0:T(8,128)(2,1)S(1)} %get-tuple-element.21), channel_id=1, source_target_pairs={{0,2},{2,4},{4,6},{6,0},{8,10},{10,12},{12,14},{14,8},{1,3},{3,5},... | collective-permute-start | bytes 786440 | tf_op jit(solution)/shard_map/ppermute | solution.py:270
  9.6 2.2 %collective-permute-start.1 = (bf16[8,128,128]{2,1,0:T(8,128)(2,1)S(1)}, bf16[8,128,128]{2,1,0:T(8,128)(2,1)S(1)}, u32[]{:S(2)}, u32[]{:S(2)}) collective-permute-start(bf16[8,128,128]{2,1,0:T(8,128)(2,1)S(1)} %get-tuple-element.22), channel_id=1, source_target_pairs={{0,6},{2,0},{4,2},{6,4},{8,14},{10,8},{12,10},{14,12},{1,7},{3,1},... | collective-permute-start | bytes 786440 | tf_op jit(solution)/shard_map/ppermute | solution.py:270
  11.8 2.3 %collective-permute-start.5 = (bf16[8,128,128]{2,1,0:T(8,128)(2,1)S(1)}, bf16[8,128,128]{2,1,0:T(8,128)(2,1)S(1)}, u32[]{:S(2)}, u32[]{:S(2)}) collective-permute-start(bf16[8,128,128]{2,1,0:T(8,128)(2,1)S(1)} %get-tuple-element.25), channel_id=1, source_target_pairs={{0,10},{2,12},{4,14},{6,8},{8,2},{10,4},{12,6},{14,0},{1,11},{3,13... | collective-permute-start | bytes 786440 | tf_op jit(solution)/shard_map/ppermute | solution.py:270
  14.1 3.4 %collective-permute-start.6 = (bf16[8,128,128]{2,1,0:T(8,128)(2,1)S(1)}, bf16[8,128,128]{2,1,0:T(8,128)(2,1)S(1)}, u32[]{:S(2)}, u32[]{:S(2)}) collective-permute-start(bf16[8,128,128]{2,1,0:T(8,128)(2,1)S(1)} %get-tuple-element.26), channel_id=1, source_target_pairs={{0,14},{2,8},{4,10},{6,12},{8,6},{10,0},{12,2},{14,4},{1,15},{3,9}... | collective-permute-start | bytes 786440 | tf_op jit(solution)/shard_map/ppermute | solution.py:270
  17.5 2.8 %collective-permute-start.7 = (bf16[8,128,128]{2,1,0:T(8,128)(2,1)S(1)}, bf16[8,128,128]{2,1,0:T(8,128)(2,1)S(1)}, u32[]{:S(2)}, u32[]{:S(2)}) collective-permute-start(bf16[8,128,128]{2,1,0:T(8,128)(2,1)S(1)} %get-tuple-element.27), channel_id=1, source_target_pairs={{0,12},{2,14},{4,8},{6,10},{8,4},{10,6},{12,0},{14,2},{1,13},{3,15... | collective-permute-start | bytes 786440 | tf_op jit(solution)/shard_map/ppermute | solution.py:270
  20.3 3.2 %collective-permute-done.x1 = bf16[8,128,128]{2,1,0:T(8,128)(2,1)S(1)} collective-permute-done((bf16[8,128,128]{2,1,0:T(8,128)(2,1)S(1)}, bf16[8,128,128]{2,1,0:T(8,128)(2,1)S(1)}, u32[]{:S(2)}, u32[]{:S(2)}) %collective-permute-start) | collective-permute-done | bytes 262176 | tf_op jit(solution)/shard_map/ppermute | solution.py:270
  23.4 3.7 %collective-permute-start.4 = (bf16[8,128,128]{2,1,0:T(8,128)(2,1)S(1)}, bf16[8,128,128]{2,1,0:T(8,128)(2,1)S(1)}, u32[]{:S(2)}, u32[]{:S(2)}) collective-permute-start(bf16[8,128,128]{2,1,0:T(8,128)(2,1)S(1)} %get-tuple-element.24), channel_id=1, source_target_pairs={{0,8},{2,10},{4,12},{6,14},{8,0},{10,2},{12,4},{14,6},{1,9},{3,11}... | collective-permute-start | bytes 786440 | tf_op jit(solution)/shard_map/ppermute | solution.py:270
  27.1 1.0 %shard_map.19.right.right0 = bf16[8,2,17,16,128]{4,3,2,1,0:T(8,128)(2,1)S(1)} custom-call(s32[2]{0:T(128)S(1)} %pad_add_fusion.refs_0_.place, bf16[8,128,128]{2,1,0:T(8,128)(2,1)S(1)} %get-tuple-element.20.x0, bf16[8,128,128]{2,1,0:T(8,128)(2,1)S(1)} %collective-permute-done.x1, bf16[8,128,128]{2,1,0:T(8,128)(2,1)S(1)} %collective-permute-done.1.x2, ...), custom_call_target="tpu_custom_call" | custom-call | flops 268435456 | bytes 1048576 | tf_op jit(solution)/shard_map/pallas_call | solution.py:41
  28.1 0.1 collective-permute-start.3
  28.2 5.2 %collective-permute-done.7.x3 = bf16[8,128,128]{2,1,0:T(8,128)(2,1)S(1)} collective-permute-done((bf16[8,128,128]{2,1,0:T(8,128)(2,1)S(1)}, bf16[8,128,128]{2,1,0:T(8,128)(2,1)S(1)}, u32[]{:S(2)}, u32[]{:S(2)}) %collective-permute-start.7) | collective-permute-done | bytes 262176 | tf_op jit(solution)/shard_map/ppermute | solution.py:270
  33.4 3.8 %collective-permute-done.4.x0 = bf16[8,128,128]{2,1,0:T(8,128)(2,1)S(1)} collective-permute-done((bf16[8,128,128]{2,1,0:T(8,128)(2,1)S(1)}, bf16[8,128,128]{2,1,0:T(8,128)(2,1)S(1)}, u32[]{:S(2)}, u32[]{:S(2)}) %collective-permute-start.4) | collective-permute-done | bytes 262176 | tf_op jit(solution)/shard_map/ppermute | solution.py:270
  37.2 1.0 %shard_map.20.right1 = bf16[8,2,17,16,128]{4,3,2,1,0:T(8,128)(2,1)S(1)} custom-call(s32[2]{0:T(128)S(1)} %pad_add_fusion.refs_0_.place, bf16[8,128,128]{2,1,0:T(8,128)(2,1)S(1)} %collective-permute-done.4.x0, bf16[8,128,128]{2,1,0:T(8,128)(2,1)S(1)} %collective-permute-done.5.x1, bf16[8,128,128]{2,1,0:T(8,128)(2,1)S(1)} %collective-permute-done.6.x2, ...), custom_call_target="tpu_custom_call" | custom-call | flops 268435456 | bytes 1048576 | tf_op jit(solution)/shard_map/pallas_call | solution.py:41
  38.2 0.1 collective-permute-start.8
  38.3 1.7 %shard_map.21 = (bf16[3,8,256,128]{3,2,1,0:T(8,128)(2,1)S(1)}, f32[8,256,128]{2,1,0:T(8,128)S(1)}, f32[256,256]{1,0:T(8,128)S(1)}) custom-call(s32[2]{0:T(128)S(1)} %pad_add_fusion.refs_0_.place, bf16[8,2,17,16,128]{4,3,2,1,0:T(8,128)(2,1)S(1)} %shard_map.19.right.right0), custom_call_target="tpu_custom_call" | custom-call | flops 536870912 | bytes 1048576 | tf_op jit(solution)/shard_map/pallas_call | solution.py:41
  40.0 2.5 %shard_map.22 = (bf16[3,8,256,128]{3,2,1,0:T(8,128)(2,1)S(1)}, f32[8,256,128]{2,1,0:T(8,128)S(1)}, f32[256,256]{1,0:T(8,128)S(1)}, f32[256,256]{1,0:T(8,128)S(1)}) custom-call(s32[2]{0:T(128)S(1)} %pad_add_fusion.refs_0_.place, bf16[8,2,17,16,128]{4,3,2,1,0:T(8,128)(2,1)S(1)} %shard_map.19.right.right0, bf16[8,2,17,16,128]{4,3,2,1,0:T(8,128)(2,1)S(1)} %shard_map.20.right1), custom_call_target="tpu_custom_call" | custom-call | flops 1073741824 | bytes 1048576 | tf_op jit(solution)/shard_map/pallas_call | solution.py:41
  42.6 1.5 %shard_map.23.b00 = f32[256,256]{1,0:T(8,128)S(1)} custom-call(s32[2]{0:T(128)S(1)} %pad_add_fusion.refs_0_.place, bf16[8,2,17,16,128]{4,3,2,1,0:T(8,128)(2,1)S(1)} %collective-permute-done.3.right.right0, bf16[3,8,256,128]{3,2,1,0:T(8,128)(2,1)S(1)} %get-tuple-element.28.left.left0, f32[8,256,128]{2,1,0:T(8,128)S(1)} %get-tuple-element.29.col_inv.col_inv0), custom_call_target="tpu_custom_call" | custom-call | flops 536870912 | bytes 1048576 | tf_op jit(solution)/shard_map/pallas_call | solution.py:41
  44.1 3.7 %shard_map.24 = f32[8,8,64,128]{3,2,1,0:T(8,128)S(1)} custom-call(s32[2]{0:T(128)S(1)} %pad_add_fusion.refs_0_.place, bf16[8,2,17,16,128]{4,3,2,1,0:T(8,128)(2,1)S(1)} %collective-permute-done.3.right.right0, bf16[8,2,17,16,128]{4,3,2,1,0:T(8,128)(2,1)S(1)} %collective-permute-done.8.right1, bf16[3,8,256,128]{3,2,1,0:T(8,128)(2,1)S(1)} %get-tuple-element.28.left.left0, ...), custom_call_target="tpu_custom_call" | custom-call | flops 1610612736 | bytes 1048576 | tf_op jit(solution)/shard_map/pallas_call | solution.py:41
  47.7 0.2 convert_element_type.9
  48.0 28.2 %all_to_all.5 = f16[64,64,128]{2,1,0:T(8,128)(2,1)S(1)} all-to-all(f16[64,64,128]{2,1,0:T(8,128)(2,1)S(1)} %bitcast.3), channel_id=1, replica_groups=mesh['band'=8,'chip'=8,'core'=2] {'chip','band'}, dimensions={0} | all-to-all | bytes 2097152 | tf_op jit(solution)/shard_map/all_to_all | solution.py:283
  76.2 1.2 %fusion.2 = f32[64,128]{1,0:T(8,128)} fusion(f16[64,64,128]{2,1,0:T(8,128)(2,1)S(1)} %all_to_all.5), kind=kLoop, calls=%fused_computation.6 | loop fusion | flops 3661824 | bytes 1081344 | tf_op jit(solution)/shard_map/reduce_sum | solution.py:285
  (6 shorter events, 0.0 us)
Async XLA Ops:
  2.4 15.0 %collective-permute-start.2 = (bf16[8,128,128]{2,1,0:T(8,128)(2,1)S(1)}, bf16[8,128,128]{2,1,0:T(8,128)(2,1)S(1)}, u32[]{:S(2)}, u32[]{:S(2)}) collective-permute-start(bf16[8,128,128]{2,1,0:T(8,128)(2,1)S(1)} %get-tuple-element.23), channel_id=1, source_target_pairs={{0,4},{2,6},{4,0},{6,2},{8,12},{10,14},{12,8},{14,10},{1,5},{3,7},... | collective-permute-start | bytes 786440 | tf_op jit(solution)/shard_map/ppermute | solution.py:270
  8.5 14.9 %collective-permute-start = (bf16[8,128,128]{2,1,0:T(8,128)(2,1)S(1)}, bf16[8,128,128]{2,1,0:T(8,128)(2,1)S(1)}, u32[]{:S(2)}, u32[]{:S(2)}) collective-permute-start(bf16[8,128,128]{2,1,0:T(8,128)(2,1)S(1)} %get-tuple-element.21), channel_id=1, source_target_pairs={{0,2},{2,4},{4,6},{6,0},{8,10},{10,12},{12,14},{14,8},{1,3},{3,5},... | collective-permute-start | bytes 786440 | tf_op jit(solution)/shard_map/ppermute | solution.py:270
  9.6 17.5 %collective-permute-start.1 = (bf16[8,128,128]{2,1,0:T(8,128)(2,1)S(1)}, bf16[8,128,128]{2,1,0:T(8,128)(2,1)S(1)}, u32[]{:S(2)}, u32[]{:S(2)}) collective-permute-start(bf16[8,128,128]{2,1,0:T(8,128)(2,1)S(1)} %get-tuple-element.22), channel_id=1, source_target_pairs={{0,6},{2,0},{4,2},{6,4},{8,14},{10,8},{12,10},{14,12},{1,7},{3,1},... | collective-permute-start | bytes 786440 | tf_op jit(solution)/shard_map/ppermute | solution.py:270
  11.8 16.4 %collective-permute-start.5 = (bf16[8,128,128]{2,1,0:T(8,128)(2,1)S(1)}, bf16[8,128,128]{2,1,0:T(8,128)(2,1)S(1)}, u32[]{:S(2)}, u32[]{:S(2)}) collective-permute-start(bf16[8,128,128]{2,1,0:T(8,128)(2,1)S(1)} %get-tuple-element.25), channel_id=1, source_target_pairs={{0,10},{2,12},{4,14},{6,8},{8,2},{10,4},{12,6},{14,0},{1,11},{3,13... | collective-permute-start | bytes 786440 | tf_op jit(solution)/shard_map/ppermute | solution.py:270
  14.1 14.1 %collective-permute-start.6 = (bf16[8,128,128]{2,1,0:T(8,128)(2,1)S(1)}, bf16[8,128,128]{2,1,0:T(8,128)(2,1)S(1)}, u32[]{:S(2)}, u32[]{:S(2)}) collective-permute-start(bf16[8,128,128]{2,1,0:T(8,128)(2,1)S(1)} %get-tuple-element.26), channel_id=1, source_target_pairs={{0,14},{2,8},{4,10},{6,12},{8,6},{10,0},{12,2},{14,4},{1,15},{3,9}... | collective-permute-start | bytes 786440 | tf_op jit(solution)/shard_map/ppermute | solution.py:270
  17.5 16.0 %collective-permute-start.7 = (bf16[8,128,128]{2,1,0:T(8,128)(2,1)S(1)}, bf16[8,128,128]{2,1,0:T(8,128)(2,1)S(1)}, u32[]{:S(2)}, u32[]{:S(2)}) collective-permute-start(bf16[8,128,128]{2,1,0:T(8,128)(2,1)S(1)} %get-tuple-element.27), channel_id=1, source_target_pairs={{0,12},{2,14},{4,8},{6,10},{8,4},{10,6},{12,0},{14,2},{1,13},{3,15... | collective-permute-start | bytes 786440 | tf_op jit(solution)/shard_map/ppermute | solution.py:270
  23.4 13.8 %collective-permute-start.4 = (bf16[8,128,128]{2,1,0:T(8,128)(2,1)S(1)}, bf16[8,128,128]{2,1,0:T(8,128)(2,1)S(1)}, u32[]{:S(2)}, u32[]{:S(2)}) collective-permute-start(bf16[8,128,128]{2,1,0:T(8,128)(2,1)S(1)} %get-tuple-element.24), channel_id=1, source_target_pairs={{0,8},{2,10},{4,12},{6,14},{8,0},{10,2},{12,4},{14,6},{1,9},{3,11}... | collective-permute-start | bytes 786440 | tf_op jit(solution)/shard_map/ppermute | solution.py:270
  28.1 14.4 %collective-permute-start.3 = (bf16[8,2,17,16,128]{4,3,2,1,0:T(8,128)(2,1)S(1)}, bf16[8,2,17,16,128]{4,3,2,1,0:T(8,128)(2,1)S(1)}, u32[]{:S(2)}, u32[]{:S(2)}) collective-permute-start(bf16[8,2,17,16,128]{4,3,2,1,0:T(8,128)(2,1)S(1)} %shard_map.19.right.right0), channel_id=1, source_target_pairs={{0,1},{1,0},{2,3},{3,2},{4,5},{5,4},{6,7},{7,6},{8,9},{9,8},{10,11... | collective-permute-start | bytes 3342344 | tf_op jit(solution)/shard_map/ppermute | solution.py:273
  38.2 5.9 %collective-permute-start.8 = (bf16[8,2,17,16,128]{4,3,2,1,0:T(8,128)(2,1)S(1)}, bf16[8,2,17,16,128]{4,3,2,1,0:T(8,128)(2,1)S(1)}, u32[]{:S(2)}, u32[]{:S(2)}) collective-permute-start(bf16[8,2,17,16,128]{4,3,2,1,0:T(8,128)(2,1)S(1)} %shard_map.20.right1), channel_id=1, source_target_pairs={{0,1},{1,0},{2,3},{3,2},{4,5},{5,4},{6,7},{7,6},{8,9},{9,8},{10,11... | collective-permute-start | bytes 3342344 | tf_op jit(solution)/shard_map/ppermute | solution.py:277
